TPU v7x, 32 devices: a whole 2x2x4 slice. The times are simulated.
32 devices in a mesh: dp: 16 (over z, x, core), tensor: 2 (over y).
Axes of the slice: x: 2, y: 2, z: 4, core: 2. Of those that a mesh axis runs over, the one named last changes fastest.
Arguments:
- tokens: bfloat16 [8192, 1536], P(('dp', 'tensor')), may hold values from -6 to 6
- out_grad: bfloat16 [8192, 1536], P(('dp', 'tensor')), may hold values from -6 to 6
- attn_norm: float32 [1536], replicated, may hold values from 0.1 to 1.9
- query_weight: bfloat16 [1536, 1536], P('dp', 'tensor')
- key_weight: bfloat16 [1536, 512], P('dp', 'tensor')
- value_weight: bfloat16 [1536, 512], P('dp', 'tensor'), may hold values from -0.15625 to 0.15625
- output_weight: bfloat16 [1536, 1536], P('dp', 'tensor'), may hold values from -0.625 to 0.625
- moe_norm: float32 [1536], replicated, may hold values from 0.1 to 1.9
- gate_weight: bfloat16 [20, 1536, 512], P(None, 'dp', 'tensor'), may hold values from -0.15625 to 0.15625
- up_weight: bfloat16 [20, 1536, 512], P(None, 'dp', 'tensor'), may hold values from -0.15625 to 0.15625
- down_weight: bfloat16 [20, 1536, 512], P(None, 'dp', 'tensor'), may hold values from -0.5 to 0.5
- expert_ids: int32 [8192, 8], P('dp'), may hold values from 0 to 19, all different within a row; in each aligned block of 512 rows (0 to 511, 512 to 1023, ...) at most 256 rows name the same one
- gate_weights: float32 [8192, 8], P('dp'), may hold values from 0.05 to 0.5
- seq_lengths: int32 [16, 4], P('dp'), may hold values from 0 to 512, as said below
Outputs:
- block_out: bfloat16 [8192, 1536], P(('dp', 'tensor'))
- input_grad: float32 [8192, 1536], P(('dp', 'tensor'))
- grad_attn_norm: float32 [1536], replicated
- grad_query: float32 [1536, 1536], P('dp', 'tensor')
- grad_key: float32 [1536, 512], P('dp', 'tensor')
- grad_value: float32 [1536, 512], P('dp', 'tensor')
- grad_output: float32 [1536, 1536], P('dp', 'tensor')
- grad_moe_norm: float32 [1536], replicated
- grad_gate: float32 [20, 1536, 512], P(None, 'dp', 'tensor')
- grad_up: float32 [20, 1536, 512], P(None, 'dp', 'tensor')
- grad_down: float32 [20, 1536, 512], P(None, 'dp', 'tensor')
Inputs may be any that keep to these rules, and one draw needn't show every extreme that they name: `seq_lengths`: each index of dp has 4 entries; a sequence of length n takes the next n rounded up to a multiple of 128 rows of that index, from its first row on, and an entry 0 takes none; the sequences of an index fill between half and all of its 512 rows, and on one index a single sequence fills all of them. `expert_ids`: within the 512 rows of one index of dp each expert is named by at most 256 rows; the 8 entries of a row differ.
All inputs are finite; a program needn't handle non-finite values.
Results may differ from a plain program's by a relative error of at most 0.024.
The roundings to bfloat16 on the way count: a program that leaves them out, or rounds other values in their place, can miss the bound.
Values may be sent and summed in bfloat16 or wider, within the bound.
A program may use at most 384 MiB of HBM per device.

v0:
```python
import math

import jax
import jax.numpy as jnp
from jax import lax
from jax.sharding import PartitionSpec as P

HEAD_DIM = 64
BLOCK = 128
CAP = 256


EPSILON = 1e-06
ROPE_BASE = 10000.0
MASKED = -1e30


def batched(pattern, first_op, second_op):
    return jnp.einsum(pattern, first_op, second_op, preferred_element_type=jnp.float32)


def times_t(first_op, weight):
    return lax.dot_general(
        first_op, weight, (((1,), (1,)), ((), ())), preferred_element_type=jnp.float32
    )


def plain_dot(first_op, weight):
    return jnp.dot(first_op, weight, preferred_element_type=jnp.float32)


def inner_rows(first_op, second_op):
    return lax.dot_general(
        first_op, second_op, (((0,), (0,)), ((), ())), preferred_element_type=jnp.float32
    )


def rms_rows(widened):
    inv_rms = lax.rsqrt(jnp.mean(widened * widened, axis=-1, keepdims=True) + EPSILON)
    return (widened * inv_rms, inv_rms)


def norm_back(grad_in, unit_rows, inv_rms, gain):
    scaled = grad_in * gain
    back = inv_rms * (scaled - unit_rows * jnp.mean(scaled * unit_rows, axis=-1, keepdims=True))
    return (back, jnp.sum(grad_in * unit_rows, axis=0))


def row_layout(lengths, row_count):
    padded = (lengths + BLOCK - 1) // BLOCK * BLOCK
    seq_ends = jnp.cumsum(padded)
    starts = seq_ends - padded
    row_ids = jnp.arange(row_count, dtype=jnp.int32)
    doc_ids = jnp.sum((row_ids[:, None] >= seq_ends[None, :]).astype(jnp.int32), axis=1)
    chosen = doc_ids[:, None] == jnp.arange(lengths.shape[0], dtype=jnp.int32)[None, :]
    first_row = jnp.sum(jnp.where(chosen, starts[None, :], 0), axis=1)
    length_row = jnp.sum(jnp.where(chosen, lengths[None, :], 0), axis=1)
    positions = row_ids - first_row
    return (doc_ids, positions, positions < length_row)


def rope_tables(positions, width):
    frequency = jnp.exp(
        jnp.arange(width // 2, dtype=jnp.int32).astype(jnp.float32)
        * (-2.0 * math.log(ROPE_BASE) / width)
    )
    angles = positions.astype(jnp.float32)[:, None] * frequency[None, :]
    cosine = jnp.cos(angles)
    sine_table = jnp.sin(angles)
    return (
        jnp.concatenate([cosine, cosine], axis=1),
        jnp.concatenate([sine_table, sine_table], axis=1),
    )


def rotate(values, cosine, sine_table):
    half_width = values.shape[-1] // 2
    turned = jnp.concatenate([-values[..., half_width:], values[..., :half_width]], axis=-1)
    return values * cosine[:, None, :] + turned * sine_table[:, None, :]


def rotate_back(grads, cosine, sine_table):
    half_width = grads.shape[-1] // 2
    turned = jnp.concatenate([grads[..., half_width:], -grads[..., :half_width]], axis=-1)
    return grads * cosine[:, None, :] + turned * sine_table[:, None, :]


def block_span(row_count):
    return min(512, row_count)


def allowed_block(first_row, block_rows, doc_ids, live_rows):
    row_count = doc_ids.shape[0]
    query_rows = first_row + jnp.arange(block_rows, dtype=jnp.int32)
    key_rows = jnp.arange(row_count, dtype=jnp.int32)
    same_doc = (key_rows[None, :] <= query_rows[:, None]) & (doc_ids[None, :] == doc_ids[:, None])
    same_doc = same_doc & live_rows[None, :] & live_rows[:, None]
    return same_doc | (key_rows[None, :] == query_rows[:, None])


def attend(queries, keys_rot, values, doc_ids, live_rows):
    row_count, head_count, head_width = queries.shape
    group_size = head_count // keys_rot.shape[1]
    keys_wide = jnp.repeat(keys_rot, group_size, axis=1)
    values_wide = jnp.repeat(values, group_size, axis=1)
    block_rows = block_span(row_count)
    block_count = row_count // block_rows
    score_scale = head_width ** (-0.5)

    def one_block(block_index):
        first_row = block_index * block_rows
        scores = batched("qhd,khd->hqk", queries, keys_wide) * score_scale
        scores = jnp.where(
            allowed_block(first_row, block_rows, doc_ids, live_rows)[None], scores, MASKED
        )
        highest = jnp.max(scores, axis=-1, keepdims=True)
        weights_exp = jnp.exp(scores - highest)
        totals = jnp.sum(weights_exp, axis=-1, keepdims=True)
        probability = (weights_exp / totals).astype(jnp.bfloat16)
        log_total = (highest + jnp.log(totals))[:, :, 0]
        return (batched("hqk,khd->qhd", probability, values_wide).astype(jnp.bfloat16), log_total)

    attn_blocks, log_totals = lax.map(one_block, jnp.arange(block_count, dtype=jnp.int32))
    return (attn_blocks.reshape(row_count, head_count, head_width), log_totals)


def attend_back(queries, keys_rot, values, attn_rows, log_totals, attn_grad, doc_ids, live_rows):
    row_count, head_count, head_width = queries.shape
    kv_count = keys_rot.shape[1]
    group_size = head_count // kv_count
    keys_wide = jnp.repeat(keys_rot, group_size, axis=1)
    values_wide = jnp.repeat(values, group_size, axis=1)
    block_rows = block_span(row_count)
    block_count = row_count // block_rows
    score_scale = head_width ** (-0.5)

    def one_block(running, block_index):
        key_acc, value_acc = running
        first_row = block_index * block_rows
        scores = batched("qhd,khd->hqk", queries, keys_wide) * score_scale
        scores = jnp.where(
            allowed_block(first_row, block_rows, doc_ids, live_rows)[None], scores, MASKED
        )
        probability = jnp.exp(scores - log_totals[block_index][:, :, None])
        value_acc = value_acc + batched("hqk,qhd->khd", probability.astype(jnp.bfloat16), attn_grad)
        through = batched("qhd,khd->hqk", attn_grad, values_wide)
        diagonal = jnp.sum(attn_grad.astype(jnp.float32) * attn_rows.astype(jnp.float32), axis=-1).T
        score_grad = (probability * (through - diagonal[:, :, None])).astype(jnp.bfloat16)
        query_grad = batched("hqk,khd->qhd", score_grad, keys_wide) * score_scale
        key_acc = key_acc + batched("hqk,qhd->khd", score_grad, queries) * score_scale
        return ((key_acc, value_acc), query_grad)

    zero_heads = jnp.zeros((row_count, head_count, head_width), jnp.float32)
    (key_acc, value_acc), query_grads = lax.scan(
        one_block, (zero_heads, zero_heads), jnp.arange(block_count, dtype=jnp.int32)
    )
    query_grad = query_grads.reshape(row_count, head_count, head_width)
    key_grad = key_acc.reshape(row_count, kv_count, group_size, head_width).sum(axis=2)
    value_grad = value_acc.reshape(row_count, kv_count, group_size, head_width).sum(axis=2)
    return (query_grad, key_grad, value_grad)


def slot_map(expert_ids, live_rows, gate_weights, expert_count, capacity):
    row_count, top_count = expert_ids.shape
    flat_ids = expert_ids.reshape(-1)
    valid_pair = jnp.repeat(live_rows, top_count)
    onehot = (
        (flat_ids[:, None] == jnp.arange(expert_count, dtype=jnp.int32)[None, :])
        & valid_pair[:, None]
    ).astype(jnp.int32)
    slot_rank = jnp.sum(jnp.cumsum(onehot, axis=0) * onehot, axis=1) - 1
    target = jnp.where(valid_pair, flat_ids * capacity + slot_rank, expert_count * capacity)
    token_rows = jnp.repeat(jnp.arange(row_count, dtype=jnp.int32), top_count)
    sources = (
        jnp.full((expert_count * capacity + 1,), row_count, jnp.int32).at[target].set(token_rows)
    )
    slot_gate = (
        jnp.zeros((expert_count * capacity + 1,), jnp.float32)
        .at[target]
        .set(gate_weights.reshape(-1))
    )
    return (
        sources[:-1].reshape(expert_count, capacity),
        slot_gate[:-1].reshape(expert_count, capacity),
    )


def silu_parts(gate_pre):
    sigma = jax.nn.sigmoid(gate_pre)
    return (gate_pre * sigma, sigma * (1.0 + gate_pre * (1.0 - sigma)))


def expert_forward(expert_in, sources, slot_gate, gate_full, up_full, down_full):
    row_count, width = expert_in.shape
    padded_rows = jnp.concatenate([expert_in, jnp.zeros((1, width), expert_in.dtype)], axis=0)

    def one_expert(accum, item):
        source_e, gate_e, gate_w, up_w, down_w = item
        rows_e = padded_rows[source_e]
        gate_pre = plain_dot(rows_e, gate_w)
        up_pre = plain_dot(rows_e, up_w)
        activ = (silu_parts(gate_pre)[0] * up_pre).astype(jnp.bfloat16)
        result = times_t(activ, down_w)
        accum = accum.at[source_e].add(result * gate_e[:, None])
        return (accum, (gate_pre, up_pre))

    accum, kept = lax.scan(
        one_expert,
        jnp.zeros((row_count + 1, width), jnp.float32),
        (sources, slot_gate, gate_full, up_full, down_full),
    )
    return (accum[:row_count], kept)


def expert_backward(expert_in, grad_rows, sources, slot_gate, gate_full, up_full, down_full, kept):
    row_count, width = expert_in.shape
    padded_rows = jnp.concatenate([expert_in, jnp.zeros((1, width), expert_in.dtype)], axis=0)
    padded_grads = jnp.concatenate([grad_rows, jnp.zeros((1, width), grad_rows.dtype)], axis=0)

    def one_expert(accum, item):
        source_e, gate_e, gate_w, up_w, down_w, gate_pre, up_pre = item
        slot_grad = (padded_grads[source_e].astype(jnp.float32) * gate_e[:, None]).astype(
            jnp.bfloat16
        )
        act_grad = plain_dot(slot_grad, down_w)
        silu_val, slope = silu_parts(gate_pre)
        activ = (silu_val * up_pre).astype(jnp.bfloat16)
        gate_grad = (act_grad * up_pre * slope).astype(jnp.bfloat16)
        up_grad = (act_grad * silu_val).astype(jnp.bfloat16)
        rows_e = padded_rows[source_e]
        grad_d = inner_rows(slot_grad, activ)
        grad_g = inner_rows(rows_e, gate_grad)
        grad_u = inner_rows(rows_e, up_grad)
        back = times_t(gate_grad, gate_w) + times_t(up_grad, up_w)
        accum = accum.at[source_e].add(back)
        return (accum, (grad_g, grad_u, grad_d))

    accum, grads = lax.scan(
        one_expert,
        jnp.zeros((row_count + 1, width), jnp.float32),
        (sources, slot_gate, gate_full, up_full, down_full, kept[0], kept[1]),
    )
    return (accum[:row_count], grads)


def local(
    tokens,
    out_grad,
    attn_norm,
    query_weight,
    key_weight,
    value_weight,
    output_weight,
    moe_norm,
    gate_weight,
    up_weight,
    down_weight,
    expert_ids,
    gate_weights,
    seq_lengths,
):
    gathered = (
        lax.all_gather(query_weight, "dp", axis=0, tiled=True),
        lax.all_gather(key_weight, "dp", axis=0, tiled=True),
        lax.all_gather(value_weight, "dp", axis=0, tiled=True),
        lax.all_gather(output_weight, "dp", axis=0, tiled=True),
        lax.all_gather(gate_weight, "dp", axis=1, tiled=True),
        lax.all_gather(up_weight, "dp", axis=1, tiled=True),
        lax.all_gather(down_weight, "dp", axis=1, tiled=True),
    )
    query_full, key_full, value_full, output_full, gate_full, up_full, down_full = gathered
    row_count = expert_ids.shape[0]
    doc_ids, positions, live_rows = row_layout(seq_lengths[0], row_count)
    cosine, sine_table = rope_tables(positions, HEAD_DIM)
    widened = tokens.astype(jnp.float32)
    unit_attn, inv_attn = rms_rows(widened)
    normed = (unit_attn * attn_norm).astype(jnp.bfloat16)
    normed_all = lax.all_gather(normed, "tensor", axis=0, tiled=True)
    head_count = query_full.shape[1] // HEAD_DIM
    kv_count = key_full.shape[1] // HEAD_DIM
    queries = rotate(
        plain_dot(normed_all, query_full).reshape(row_count, head_count, HEAD_DIM),
        cosine,
        sine_table,
    ).astype(jnp.bfloat16)
    keys_rot = rotate(
        plain_dot(normed_all, key_full).reshape(row_count, kv_count, HEAD_DIM), cosine, sine_table
    ).astype(jnp.bfloat16)
    values = (
        plain_dot(normed_all, value_full)
        .astype(jnp.bfloat16)
        .reshape(row_count, kv_count, HEAD_DIM)
    )
    attn_rows, log_totals = attend(queries, keys_rot, values, doc_ids, live_rows)
    attn_flat = attn_rows.reshape(row_count, head_count * HEAD_DIM)
    after_attn = widened + lax.psum_scatter(
        times_t(attn_flat, output_full).astype(jnp.bfloat16),
        "tensor",
        scatter_dimension=0,
        tiled=True,
    ).astype(jnp.float32)
    unit_moe, inv_moe = rms_rows(after_attn)
    expert_in = (unit_moe * moe_norm).astype(jnp.bfloat16)
    expert_all = lax.all_gather(expert_in, "tensor", axis=0, tiled=True)
    sources, slot_gate = slot_map(expert_ids, live_rows, gate_weights, gate_full.shape[0], CAP)
    mix_part, kept = expert_forward(expert_all, sources, slot_gate, gate_full, up_full, down_full)
    mixed = lax.psum_scatter(
        mix_part.astype(jnp.bfloat16), "tensor", scatter_dimension=0, tiled=True
    ).astype(jnp.float32)
    block_out = (after_attn + mixed).astype(jnp.bfloat16)
    grad_all = lax.all_gather(out_grad, "tensor", axis=0, tiled=True)
    moe_part, expert_grads = expert_backward(
        expert_all, grad_all, sources, slot_gate, gate_full, up_full, down_full, kept
    )
    moe_grad = lax.psum_scatter(
        moe_part.astype(jnp.bfloat16), "tensor", scatter_dimension=0, tiled=True
    ).astype(jnp.float32)
    back_moe, grad_moe_norm = norm_back(moe_grad, unit_moe, inv_moe, moe_norm)
    resid_grad = out_grad.astype(jnp.float32) + back_moe
    resid_half = resid_grad.astype(jnp.bfloat16)
    resid_all = lax.all_gather(resid_half, "tensor", axis=0, tiled=True)
    grad_output = inner_rows(resid_all, attn_flat)
    attn_grad = (
        plain_dot(resid_all, output_full)
        .astype(jnp.bfloat16)
        .reshape(row_count, head_count, HEAD_DIM)
    )
    query_grad, key_grad, value_grad = attend_back(
        queries, keys_rot, values, attn_rows, log_totals, attn_grad, doc_ids, live_rows
    )
    query_pre = (
        rotate_back(query_grad, cosine, sine_table).astype(jnp.bfloat16).reshape(row_count, -1)
    )
    key_pre = rotate_back(key_grad, cosine, sine_table).astype(jnp.bfloat16).reshape(row_count, -1)
    value_pre = value_grad.astype(jnp.bfloat16).reshape(row_count, -1)
    grad_query = inner_rows(normed_all, query_pre)
    grad_key = inner_rows(normed_all, key_pre)
    grad_value = inner_rows(normed_all, value_pre)
    attn_in_grad = lax.psum_scatter(
        (
            times_t(query_pre, query_full)
            + times_t(key_pre, key_full)
            + times_t(value_pre, value_full)
        ).astype(jnp.bfloat16),
        "tensor",
        scatter_dimension=0,
        tiled=True,
    ).astype(jnp.float32)
    back_attn, grad_attn_norm = norm_back(attn_in_grad, unit_attn, inv_attn, attn_norm)
    input_grad = resid_grad + back_attn
    gain_sums = lax.psum((grad_attn_norm, grad_moe_norm), ("dp", "tensor"))
    summed = (
        lax.psum_scatter(grad_query, "dp", scatter_dimension=0, tiled=True),
        lax.psum_scatter(grad_key, "dp", scatter_dimension=0, tiled=True),
        lax.psum_scatter(grad_value, "dp", scatter_dimension=0, tiled=True),
        lax.psum_scatter(grad_output, "dp", scatter_dimension=0, tiled=True),
        lax.psum_scatter(expert_grads[0], "dp", scatter_dimension=1, tiled=True),
        lax.psum_scatter(expert_grads[1], "dp", scatter_dimension=1, tiled=True),
        lax.psum_scatter(expert_grads[2], "dp", scatter_dimension=1, tiled=True),
    )
    return (
        block_out,
        input_grad,
        gain_sums[0],
        summed[0],
        summed[1],
        summed[2],
        summed[3],
        gain_sums[1],
        summed[4],
        summed[5],
        summed[6],
    )


def solution(mesh):
    in_specs = (
        P(("dp", "tensor"), None),
        P(("dp", "tensor"), None),
        P(),
        P("dp", "tensor"),
        P("dp", "tensor"),
        P("dp", "tensor"),
        P("dp", "tensor"),
        P(),
        P(None, "dp", "tensor"),
        P(None, "dp", "tensor"),
        P(None, "dp", "tensor"),
        P("dp", None),
        P("dp", None),
        P("dp", None),
    )
    out_specs = (
        P(("dp", "tensor"), None),
        P(("dp", "tensor"), None),
        P(),
        P("dp", "tensor"),
        P("dp", "tensor"),
        P("dp", "tensor"),
        P("dp", "tensor"),
        P(),
        P(None, "dp", "tensor"),
        P(None, "dp", "tensor"),
        P(None, "dp", "tensor"),
    )
    return jax.shard_map(local, mesh=mesh, in_specs=in_specs, out_specs=out_specs, check_vma=False)
```

profile of v0, /device:TPU:0, one launch (start us, length us, event | category | flops | bytes accessed | tf_op | source)
XLA Modules:
  0.0 2738.6 jit_solution(8027386978782775603)
XLA Ops:
  14.8 25.5 all_gather.36
  40.3 20.3 all_gather.34
  64.9 22.1 all-gather.12.cloned.1.call-done
  101.4 29.0 %all-gather.14.cloned.1.call-done = bf16[1536,768]{1,0:T(8,128)(2,1)} async-done(((bf16[96,768]{1,0:T(8,128)(2,1)}), bf16[1536,768]{1,0:T(8,128)(2,1)}) %all-gather.14.cloned.1.call-update) | async-done | bytes 2359312 | tf_op jit(solution)/shard_map/all_gather | solution.py:266
  135.3 12.4 all-gather.16.cloned.1.call-start
  147.7 12.0 reduce-scatter.12.cloned.1.call-done
  174.1 15.5 scatter_custom_fusion.2
  189.7 15.5 scatter_custom_fusion.3
  206.8 10.7 all-gather.16.cloned.1.call-done
  219.0 120.7 %all-gather.18.cloned.1.call-done = bf16[20,1536,256]{2,1,0:T(8,128)(2,1)} async-done(((bf16[20,96,256]{2,1,0:T(8,128)(2,1)}), bf16[20,1536,256]{2,1,0:T(8,128)(2,1)}) %all-gather.18.cloned.1.call-update) | async-done | bytes 15728656 | tf_op jit(solution)/shard_map/all_gather | solution.py:267
  339.7 120.3 %all-gather.20.cloned.1.call-done = bf16[20,1536,256]{2,1,0:T(8,128)(2,1)} async-done(((bf16[20,96,256]{2,1,0:T(8,128)(2,1)}), bf16[20,1536,256]{2,1,0:T(8,128)(2,1)}) %all-gather.20.cloned.1.call-update) | async-done | bytes 15728656 | tf_op jit(solution)/shard_map/all_gather | solution.py:268
  460.1 120.4 %all-gather.22.cloned.1.call-done = bf16[20,1536,256]{2,1,0:T(8,128)(2,1)} async-done(((bf16[20,96,256]{2,1,0:T(8,128)(2,1)}), bf16[20,1536,256]{2,1,0:T(8,128)(2,1)}) %all-gather.22.cloned.1.call-update) | async-done | bytes 15728656 | tf_op jit(solution)/shard_map/all_gather | solution.py:269
  582.5 340.9 %while.6 = (s32[]{:T(128)}, f32[513,1536]{1,0:T(8,128)}, f32[20,256,256]{2,1,0:T(8,128)}, f32[20,256,256]{2,1,0:T(8,128)}, s32[20,256]{1,0:T(8,128)S(1)}, /*inde...) while((s32[]{:T(128)}, f32[513,1536]{1,0:T(8,128)}, ...), condition=%wide.region_16.17_spmd, body=%wide.region_14.16_spmd.sunk | while | flops 605161216 | bytes 16529565 | solution.py:207
  592.1 7.4 scatter_fusion
  609.2 7.4 scatter_fusion
  626.2 7.4 scatter_fusion
  643.3 7.4 scatter_fusion
  660.3 7.4 scatter_fusion
  677.4 7.4 scatter_fusion
  694.4 7.4 scatter_fusion
  711.5 7.4 scatter_fusion
  728.5 7.4 scatter_fusion
  745.6 7.4 scatter_fusion
  762.6 7.4 scatter_fusion
  779.6 7.4 scatter_fusion
  796.7 7.4 scatter_fusion
  813.8 7.4 scatter_fusion
  830.8 7.4 scatter_fusion
  847.8 7.4 scatter_fusion
  864.9 7.4 scatter_fusion
  881.9 7.4 scatter_fusion
  899.0 7.4 scatter_fusion
  916.0 7.4 scatter_fusion
  925.5 481.9 %while.7 = (s32[]{:T(128)}, f32[513,1536]{1,0:T(8,128)}, f32[20,1536,256]{2,1,0:T(8,128)}, f32[20,1536,256]{2,1,0:T(8,128)}, f32[20,1536,256]{2,1,0:T(8,128)}, /...) while((s32[]{:T(128)}, f32[513,1536]{1,0:T(8,128)}, ...), condition=%wide.region_20.21_spmd, body=%wide.region_18.20_spmd.sunk | while | flops 1212352256 | bytes 27803848 | solution.py:238
  936.0 7.4 scatter_fusion.1
  960.1 7.4 scatter_fusion.1
  984.1 7.4 scatter_fusion.1
  1008.2 7.4 scatter_fusion.1
  1032.3 7.4 scatter_fusion.1
  1056.4 7.4 scatter_fusion.1
  1080.5 7.4 scatter_fusion.1
  1104.5 7.4 scatter_fusion.1
  1128.7 7.4 scatter_fusion.1
  1152.8 7.4 scatter_fusion.1
  1176.9 7.4 scatter_fusion.1
  1201.1 7.4 scatter_fusion.1
  1225.2 7.4 scatter_fusion.1
  1249.2 7.4 scatter_fusion.1
  1273.3 7.4 scatter_fusion.1
  1297.4 7.4 scatter_fusion.1
  1321.5 7.4 scatter_fusion.1
  1345.6 7.4 scatter_fusion.1
  1369.6 7.4 scatter_fusion.1
  1410.7 24.5 reduce-scatter.16.cloned.1.call-done
  1439.2 26.8 all-gather.26.cloned.1.call-done
  1472.2 7.4 fusion.43
  1535.6 39.9 %all-reduce.2 = (f32[1536]{0:T(1024)}, f32[1536]{0:T(1024)}) all-reduce(f32[1536]{0:T(1024)S(1)} %get-tuple-element.209, f32[1536]{0:T(1024)S(1)} %get-tuple-element.207), channel_id=1, replica_groups=mesh['dp'=16,'tensor'=2] {'dp','tensor'}, use_global_device_ids=true, to_apply=%region_29.30 | all-reduce | flops 3072 | bytes 24576 | tf_op jit(solution)/shard_map/psum | solution.py:351
  1579.5 46.7 %reduce-scatter.24.cloned.1.call-done = f32[96,256]{1,0:T(8,128)} async-done(((f32[1536,256]{1,0:T(8,128)}), f32[96,256]{1,0:T(8,128)}) %reduce-scatter.24.cloned.1.call-update) | async-done | bytes 98320 | tf_op jit(solution)/shard_map/reduce_scatter | solution.py:355
  1626.2 62.6 %reduce-scatter.22.cloned.1.call-done = f32[96,256]{1,0:T(8,128)} async-done(((f32[1536,256]{1,0:T(8,128)}), f32[96,256]{1,0:T(8,128)}) %reduce-scatter.22.cloned.1.call-update) | async-done | bytes 98320 | tf_op jit(solution)/shard_map/reduce_scatter | solution.py:354
  1688.8 78.9 %reduce-scatter.20.cloned.1.call-done = f32[96,768]{1,0:T(8,128)} async-done(((f32[1536,768]{1,0:T(8,128)}), f32[96,768]{1,0:T(8,128)}) %reduce-scatter.20.cloned.1.call-update) | async-done | bytes 294928 | tf_op jit(solution)/shard_map/reduce_scatter | solution.py:353
  1767.7 79.1 %reduce-scatter.26.cloned.1.call-done = f32[96,768]{1,0:T(8,128)} async-done(((f32[1536,768]{1,0:T(8,128)}), f32[96,768]{1,0:T(8,128)}) %reduce-scatter.26.cloned.1.call-update) | async-done | bytes 294928 | tf_op jit(solution)/shard_map/reduce_scatter | solution.py:356
  1846.8 295.0 %reduce-scatter.32.cloned.1.call-done = f32[20,96,256]{2,1,0:T(8,128)} async-done(((f32[20,1536,256]{2,1,0:T(8,128)}), f32[20,96,256]{2,1,0:T(8,128)}) %reduce-scatter.32.cloned.1.call-update) | async-done | bytes 1966096 | tf_op jit(solution)/shard_map/reduce_scatter | solution.py:359
  2141.8 295.0 %reduce-scatter.28.cloned.1.call-done = f32[20,96,256]{2,1,0:T(8,128)} async-done(((f32[20,1536,256]{2,1,0:T(8,128)}), f32[20,96,256]{2,1,0:T(8,128)}) %reduce-scatter.28.cloned.1.call-update) | async-done | bytes 1966096 | tf_op jit(solution)/shard_map/reduce_scatter | solution.py:357
  2436.7 294.8 %reduce-scatter.30.cloned.1.call-done = f32[20,96,256]{2,1,0:T(8,128)} async-done(((f32[20,1536,256]{2,1,0:T(8,128)}), f32[20,96,256]{2,1,0:T(8,128)}) %reduce-scatter.30.cloned.1.call-update) | async-done | bytes 1966096 | tf_op jit(solution)/shard_map/reduce_scatter | solution.py:358
  (691 shorter events, 658.1 us)
Async XLA Ops:
  7.2 5.8 copy-start.53
  7.2 53.4 %all-gather.10.cloned.1.call-start = ((), (), s32[]{:S(2)}) async-start(), calls=%async_computation.11 | async-start | bytes 2359296 | tf_op jit(solution)/shard_map/all_gather | solution.py:278
  9.2 5.6 copy-start.44
  11.4 28.8 %copy-start.45 = (bf16[96,256]{1,0:T(8,128)(2,1)S(1)}, bf16[96,256]{1,0:T(8,128)(2,1)}, u32[]{:S(2)}) copy-start(bf16[96,256]{1,0:T(8,128)(2,1)} %param.23) | copy-start | bytes 147460
  11.5 75.6 %all-gather.12.cloned.1.call-start = ((), (), s32[]{:S(2)}) async-start(), calls=%async_computation.12 | async-start | bytes 2506752 | tf_op jit(solution)/shard_map/all_gather | solution.py:263
  12.2 118.2 %all-gather.14.cloned.1.call-start = ((), (), s32[]{:S(2)}) async-start(), calls=%async_computation.13 | async-start | bytes 2506752 | tf_op jit(solution)/shard_map/all_gather | solution.py:266
  13.0 146.7 %reduce-scatter.12.cloned.1.call-start = ((), (), s32[]{:S(2)}) async-start(), calls=%async_computation.14 | async-start | bytes 2359296 | tf_op jit(solution)/shard_map/reduce_scatter | solution.py:296
  13.8 76.5 %copy-start.21 = (f32[512,64]{0,1:T(8,128)}, f32[512,64]{0,1:T(8,128)S(1)}, u32[]{:S(2)}) copy-start(f32[512,64]{0,1:T(8,128)S(1)} %pad_maximum_fusion.1) | copy-start | bytes 393220
  14.5 75.8 %copy-start.34 = (f32[512,64]{0,1:T(8,128)}, f32[512,64]{0,1:T(8,128)S(1)}, u32[]{:S(2)}) copy-start(f32[512,64]{0,1:T(8,128)S(1)} %get-tuple-element.280) | copy-start | bytes 393220
  14.8 80.9 %copy-start.31 = (pred[512,512]{0,1:T(8,128)(4,1)}, pred[512,512]{0,1:T(8,128)(4,1)S(1)}, u32[]{:S(2)}) copy-start(pred[512,512]{0,1:T(8,128)(4,1)S(1)} %fusion.74) | copy-start | bytes 786436
  40.2 20.3 copy-start.15
  93.0 4.5 copy-start.2
  93.0 4.7 copy-start.37
  95.7 5.7 copy-start.35
  101.4 29.0 %copy-start.24 = (bf16[12,64,512]{2,1,0:T(8,128)(2,1)}, bf16[12,64,512]{2,1,0:T(8,128)(2,1)S(1)}, u32[]{:S(2)}) copy-start(bf16[12,64,512]{2,1,0:T(8,128)(2,1)S(1)} %fusion.69) | copy-start | bytes 2359300
  134.6 25.1 copy-start.3
  134.7 26.6 copy-start.39
  134.7 70.6 %all-gather.24.cloned.1.call-start = ((), (), s32[]{:S(2)}) async-start(), calls=%async_computation.20 | async-start | bytes 2359296 | tf_op jit(solution)/shard_map/all_gather | solution.py:311
  135.3 82.3 %all-gather.16.cloned.1.call-start = ((), (), s32[]{:S(2)}) async-start(), calls=%async_computation.15 | async-start | bytes 2359296 | tf_op jit(solution)/shard_map/all_gather | solution.py:304
  161.3 1275.8 %copy-start.46 = (f32[256]{0:T(256)}, f32[256]{0:T(256)S(1)}, u32[]{:S(2)}) copy-start(f32[256]{0:T(256)S(1)} %add_rsqrt_fusion) | copy-start | bytes 3076
  162.5 177.2 %all-gather.18.cloned.1.call-start = ((), (), s32[]{:S(2)}) async-start(), calls=%async_computation.16 | async-start | bytes 16711680 | tf_op jit(solution)/shard_map/all_gather | solution.py:267
  163.3 296.8 %all-gather.20.cloned.1.call-start = ((), (), s32[]{:S(2)}) async-start(), calls=%async_computation.17 | async-start | bytes 16711680 | tf_op jit(solution)/shard_map/all_gather | solution.py:268
  164.0 416.4 %all-gather.22.cloned.1.call-start = ((), (), s32[]{:S(2)}) async-start(), calls=%async_computation.18 | async-start | bytes 16711680 | tf_op jit(solution)/shard_map/all_gather | solution.py:269
  164.8 1270.4 %reduce-scatter.16.cloned.1.call-start = ((), (), s32[]{:S(2)}) async-start(), calls=%async_computation.21 | async-start | bytes 2359296 | tf_op jit(solution)/shard_map/reduce_scatter | solution.py:315
  943.3 3.1 copy-start
  991.5 3.0 copy-start
  1015.6 3.1 copy-start
  1063.8 3.0 copy-start
  1087.9 3.0 copy-start
  1111.9 3.1 copy-start
  1136.1 3.0 copy-start
  1160.1 3.0 copy-start
  1184.3 3.2 copy-start
  1208.5 3.0 copy-start
  1256.6 3.0 copy-start
  1280.6 3.0 copy-start
  1304.7 3.0 copy-start
  1328.8 3.1 copy-start
  1377.0 3.1 copy-start
  1401.2 3.0 copy-start
  1410.6 24.6 copy-start.4
  1410.6 24.6 copy-start.8
  1410.6 26.5 copy-start.13
  1410.6 55.4 %all-gather.26.cloned.1.call-start = ((), (), s32[]{:S(2)}) async-start(), calls=%async_computation.22 | async-start | bytes 2359296 | tf_op jit(solution)/shard_map/all_gather | solution.py:321
  1438.7 95.1 %reduce-scatter.18.cloned.1.call-start = ((), (), s32[]{:S(2)}) async-start(), calls=%async_computation.23 | async-start | bytes 2359296 | tf_op jit(solution)/shard_map/reduce_scatter | solution.py:339
  1472.2 7.5 copy-start.36
  1479.7 7.1 copy-start.10
  1486.8 3.2 copy-start.12
  1495.2 4.4 copy-start.22
  1497.1 3.9 copy-start.19
  1507.5 68.0 %reduce-scatter.14.cloned.1.call-start = ((), (), s32[]{:S(2)}) async-start(), calls=%async_computation.19 | async-start | bytes 2359296 | tf_op jit(solution)/shard_map/reduce_scatter | solution.py:307
  1510.8 115.4 %reduce-scatter.24.cloned.1.call-start = ((), (), s32[]{:S(2)}) async-start(), calls=%async_computation.26 | async-start | bytes 1671168 | tf_op jit(solution)/shard_map/reduce_scatter | solution.py:355
  1514.9 173.9 %reduce-scatter.22.cloned.1.call-start = ((), (), s32[]{:S(2)}) async-start(), calls=%async_computation.25 | async-start | bytes 1671168 | tf_op jit(solution)/shard_map/reduce_scatter | solution.py:354
  1516.9 250.8 %reduce-scatter.20.cloned.1.call-start = ((), (), s32[]{:S(2)}) async-start(), calls=%async_computation.24 | async-start | bytes 5013504 | tf_op jit(solution)/shard_map/reduce_scatter | solution.py:353
  1521.8 324.9 %reduce-scatter.26.cloned.1.call-start = ((), (), s32[]{:S(2)}) async-start(), calls=%async_computation.27 | async-start | bytes 5013504 | tf_op jit(solution)/shard_map/reduce_scatter | solution.py:356
  1527.9 613.8 %reduce-scatter.32.cloned.1.call-start = ((), (), s32[]{:S(2)}) async-start(), calls=%async_computation.30 | async-start | bytes 33423360 | tf_op jit(solution)/shard_map/reduce_scatter | solution.py:359
  1528.5 908.2 %reduce-scatter.28.cloned.1.call-start = ((), (), s32[]{:S(2)}) async-start(), calls=%async_computation.28 | async-start | bytes 33423360 | tf_op jit(solution)/shard_map/reduce_scatter | solution.py:357
  1529.3 1202.3 %reduce-scatter.30.cloned.1.call-start = ((), (), s32[]{:S(2)}) async-start(), calls=%async_computation.29 | async-start | bytes 33423360 | tf_op jit(solution)/shard_map/reduce_scatter | solution.py:358
  1529.3 4.5 copy-start.42
  1529.3 4.5 copy-start.50
  1529.8 45.6 %copy-start.14 = (bf16[256,1536]{1,0:T(8,128)(2,1)S(1)}, bf16[256,1536]{1,0:T(8,128)(2,1)}, u32[]{:S(2)}) copy-start(bf16[256,1536]{1,0:T(8,128)(2,1)} %param.19) | copy-start | bytes 2359300
  1529.9 45.6 %copy-start.18 = (bf16[256,1536]{1,0:T(8,128)(2,1)S(1)}, bf16[256,1536]{1,0:T(8,128)(2,1)}, u32[]{:S(2)}) copy-start(bf16[256,1536]{1,0:T(8,128)(2,1)} %reduce-scatter.16.cloned.1.call-done) | copy-start | bytes 2359300
  1529.9 45.6 %copy-start.47 = (f32[256]{0:T(256)S(1)}, f32[256]{0:T(256)}, u32[]{:S(2)}) copy-start(f32[256]{0:T(256)} %copy-done.46) | copy-start | bytes 3076
  1529.9 45.6 %copy-start.52 = (f32[256]{0:T(256)S(1)}, f32[256]{0:T(256)}, u32[]{:S(2)}) copy-start(f32[256]{0:T(256)} %copy-done.51) | copy-start | bytes 3076
  (49 other events, 106.3 us)
Sparse Core Ops, SparseCore 0:
  11.6 29.8 all-gather.9
  43.8 43.1 all-gather.11
  89.3 41.0 all-gather.13
  134.8 24.8 reduce-scatter.11
  161.1 27.1 all-gather.23
  190.3 27.1 all-gather.15
  219.8 119.8 all-gather.17
  342.0 118.0 all-gather.19
  462.3 118.0 all-gather.21
  1410.7 24.3 reduce-scatter.15
  1438.8 27.1 all-gather.25
  1507.6 26.1 reduce-scatter.17
  1536.0 26.5 reduce-scatter.13
  1566.7 59.4 reduce-scatter.23
  1630.3 58.4 reduce-scatter.21
  1693.1 74.5 reduce-scatter.19
  1771.9 74.7 reduce-scatter.25
  1851.3 290.4 reduce-scatter.31
  2146.4 290.2 reduce-scatter.27
  2441.3 290.2 reduce-scatter.29
where the time goes:
time: 2760 us; the launch traced here: 2740 us
  waiting for transfers between devices  1650 us (60%)
  matrix products  454 us (16%)
  other arithmetic  334 us (12%)
  local copies, waits for them, and re-layouts  187 us (7%)
  blocking collectives  85.6 us (3%)
    reduce_scatter x1, waiting for transfers between devices, local(): lax.psum_scatter(expert_grads[0], 'dp', scatter_dimension=1, tiled=True)  295 us
    reduce_scatter x1, waiting for transfers between devices, local(): lax.psum_scatter(expert_grads[2], 'dp', scatter_dimension=1, tiled=True)  295 us
    reduce_scatter x1, waiting for transfers between devices, local(): lax.psum_scatter(expert_grads[1], 'dp', scatter_dimension=1, tiled=True)  295 us
    scatter-add x20, other arithmetic, one_expert(): accum = accum.at[source_e].add(result * gate_e[:, None])  149 us
    scatter-add x20, other arithmetic, one_expert(): accum = accum.at[source_e].add(back)  148 us
    dot_general x64, matrix products, times_t(): lax.dot_general(first_op, weight, (((1,), (1,)), ((), ())), preferred_ele...  146 us
    dot_general x64, matrix products, plain_dot(): return jnp.dot(first_op, weight, preferred_element_type=jnp.float32)  144 us
    dot_general x64, matrix products, inner_rows(): lax.dot_general(first_op, second_op, (((0,), (0,)), ((), ())), preferred_...  138 us
  transfers between devices with their start and end apart: 20, of which 17 were waited for; matrix products, arithmetic and copies ran while one was open for 3% of the time, Pallas kernels for 0%

commit v1 on v0

--- a/solution.py
+++ b/solution.py
@@ -1,13 +1,17 @@
+import functools
 import math
 
 import jax
 import jax.numpy as jnp
 from jax import lax
+from jax.experimental import pallas as pl
+from jax.experimental.pallas import tpu as pltpu
 from jax.sharding import PartitionSpec as P
 
 HEAD_DIM = 64
 BLOCK = 128
-CAP = 256
+GATHERS = 2
+PASSES = 4
 
 
 EPSILON = 1e-06
@@ -160,87 +164,175 @@
     return (query_grad, key_grad, value_grad)
 
 
-def slot_map(expert_ids, live_rows, gate_weights, expert_count, capacity):
-    row_count, top_count = expert_ids.shape
-    flat_ids = expert_ids.reshape(-1)
-    valid_pair = jnp.repeat(live_rows, top_count)
-    onehot = (
-        (flat_ids[:, None] == jnp.arange(expert_count, dtype=jnp.int32)[None, :])
-        & valid_pair[:, None]
-    ).astype(jnp.int32)
-    slot_rank = jnp.sum(jnp.cumsum(onehot, axis=0) * onehot, axis=1) - 1
-    target = jnp.where(valid_pair, flat_ids * capacity + slot_rank, expert_count * capacity)
-    token_rows = jnp.repeat(jnp.arange(row_count, dtype=jnp.int32), top_count)
-    sources = (
-        jnp.full((expert_count * capacity + 1,), row_count, jnp.int32).at[target].set(token_rows)
-    )
-    slot_gate = (
-        jnp.zeros((expert_count * capacity + 1,), jnp.float32)
-        .at[target]
-        .set(gate_weights.reshape(-1))
-    )
-    return (
-        sources[:-1].reshape(expert_count, capacity),
-        slot_gate[:-1].reshape(expert_count, capacity),
-    )
-
-
 def silu_parts(gate_pre):
     sigma = jax.nn.sigmoid(gate_pre)
     return (gate_pre * sigma, sigma * (1.0 + gate_pre * (1.0 - sigma)))
 
 
-def expert_forward(expert_in, sources, slot_gate, gate_full, up_full, down_full):
-    row_count, width = expert_in.shape
-    padded_rows = jnp.concatenate([expert_in, jnp.zeros((1, width), expert_in.dtype)], axis=0)
-
-    def one_expert(accum, item):
-        source_e, gate_e, gate_w, up_w, down_w = item
-        rows_e = padded_rows[source_e]
-        gate_pre = plain_dot(rows_e, gate_w)
-        up_pre = plain_dot(rows_e, up_w)
-        activ = (silu_parts(gate_pre)[0] * up_pre).astype(jnp.bfloat16)
-        result = times_t(activ, down_w)
-        accum = accum.at[source_e].add(result * gate_e[:, None])
-        return (accum, (gate_pre, up_pre))
-
-    accum, kept = lax.scan(
-        one_expert,
-        jnp.zeros((row_count + 1, width), jnp.float32),
-        (sources, slot_gate, gate_full, up_full, down_full),
-    )
-    return (accum[:row_count], kept)
-
-
-def expert_backward(expert_in, grad_rows, sources, slot_gate, gate_full, up_full, down_full, kept):
-    row_count, width = expert_in.shape
-    padded_rows = jnp.concatenate([expert_in, jnp.zeros((1, width), expert_in.dtype)], axis=0)
-    padded_grads = jnp.concatenate([grad_rows, jnp.zeros((1, width), grad_rows.dtype)], axis=0)
-
-    def one_expert(accum, item):
-        source_e, gate_e, gate_w, up_w, down_w, gate_pre, up_pre = item
-        slot_grad = (padded_grads[source_e].astype(jnp.float32) * gate_e[:, None]).astype(
-            jnp.bfloat16
+def expert_gates(expert_ids, gate_weights, live_rows, expert_count):
+    named = expert_ids[:, :, None] == jnp.arange(expert_count, dtype=jnp.int32)[None, None, :]
+    named = named & live_rows[:, None, None]
+    return jnp.sum(jnp.where(named, gate_weights[:, :, None], 0.0), axis=1)
+
+
+def expert_kernel(
+    first_expert,
+    row_tile,
+    feat_tile,
+    rows_ref,
+    rows_t_ref,
+    grads_ref,
+    grads_t_ref,
+    gates_ref,
+    gates_t_ref,
+    weights_ref,
+    mix_in_ref,
+    back_in_ref,
+    mix_ref,
+    back_ref,
+    out_ref,
+    act_ref,
+    pair_ref,
+):
+    step = pl.program_id(0)
+    expert = first_expert + step
+    row_count, width = rows_ref.shape
+    depth, hidden = weights_ref.shape[3:]
+
+    @pl.when(step == 0)
+    def _():
+        mix_ref[...] = mix_in_ref[...]
+        back_ref[...] = back_in_ref[...]
+
+    gate_w = weights_ref[:, 0, 0].reshape(width, hidden)
+    up_w = weights_ref[:, 1, 0].reshape(width, hidden)
+    down_w = weights_ref[:, 2, 0].reshape(width, hidden)
+    lanes = lax.broadcasted_iota(jnp.int32, (row_tile, gates_ref.shape[1]), 1)
+    for start in range(0, row_count, row_tile):
+        rows = slice(start, start + row_tile)
+        gate_col = jnp.sum(
+            jnp.where(lanes == expert, gates_ref[rows, :], 0.0), axis=1, keepdims=True
         )
-        act_grad = plain_dot(slot_grad, down_w)
+        gate_pre = plain_dot(rows_ref[rows, :], gate_w)
+        up_pre = plain_dot(rows_ref[rows, :], up_w)
         silu_val, slope = silu_parts(gate_pre)
         activ = (silu_val * up_pre).astype(jnp.bfloat16)
+        act_ref[rows, :] = activ
+        slot_grad = (grads_ref[rows, :].astype(jnp.float32) * gate_col).astype(jnp.bfloat16)
+        act_grad = plain_dot(slot_grad, down_w)
         gate_grad = (act_grad * up_pre * slope).astype(jnp.bfloat16)
         up_grad = (act_grad * silu_val).astype(jnp.bfloat16)
-        rows_e = padded_rows[source_e]
-        grad_d = inner_rows(slot_grad, activ)
-        grad_g = inner_rows(rows_e, gate_grad)
-        grad_u = inner_rows(rows_e, up_grad)
-        back = times_t(gate_grad, gate_w) + times_t(up_grad, up_w)
-        accum = accum.at[source_e].add(back)
-        return (accum, (grad_g, grad_u, grad_d))
-
-    accum, grads = lax.scan(
-        one_expert,
-        jnp.zeros((row_count + 1, width), jnp.float32),
-        (sources, slot_gate, gate_full, up_full, down_full, kept[0], kept[1]),
-    )
-    return (accum[:row_count], grads)
+        pair_ref[rows, :hidden] = gate_grad
+        pair_ref[rows, hidden:] = up_grad
+        mix_ref[rows, :] += times_t(activ, down_w) * gate_col
+        back_ref[rows, :] += times_t(gate_grad, gate_w) + times_t(up_grad, up_w)
+    gate_row = gates_t_ref[pl.ds(expert, 1), :]
+    per_tile = feat_tile // depth
+    for tile in range(width // feat_tile):
+        feats = slice(tile * feat_tile, (tile + 1) * feat_tile)
+        parts = slice(tile * per_tile, (tile + 1) * per_tile)
+        pair = plain_dot(rows_t_ref[feats, :], pair_ref[...]).astype(jnp.bfloat16)
+        out_ref[parts, 0, 0] = pair[:, :hidden].reshape(per_tile, depth, hidden)
+        out_ref[parts, 1, 0] = pair[:, hidden:].reshape(per_tile, depth, hidden)
+        slot_grad_t = (grads_t_ref[feats, :].astype(jnp.float32) * gate_row).astype(jnp.bfloat16)
+        down = plain_dot(slot_grad_t, act_ref[...]).astype(jnp.bfloat16)
+        out_ref[parts, 2, 0] = down.reshape(per_tile, depth, hidden)
+
+
+def expert_pass(first_expert, count, offset, rows, rows_t, grads, grads_t, gates, gates_t, weights, mix, back):
+    shards, kinds, held, depth, hidden = weights.shape
+    row_count, width = rows.shape
+    packed = depth % 16 != 0
+    if packed:
+        weights = weights.transpose(1, 2, 0, 3, 4).reshape(1, kinds, held, width, hidden)
+    groups, inner = weights.shape[0], weights.shape[3]
+    feat_tile = inner
+    while feat_tile < 384 and (width // feat_tile) % 2 == 0:
+        feat_tile *= 2
+
+    def whole(array):
+        return pl.BlockSpec(array.shape, lambda i: (0,) * array.ndim, pipeline_mode=pl.Buffered(1))
+
+    shape = (groups, kinds, 1, inner, hidden)
+    block = pl.BlockSpec(shape, lambda i: (0, 0, i + offset, 0, 0))
+    out_block = pl.BlockSpec(shape, lambda i: (0, 0, i, 0, 0))
+    fixed = (rows, rows_t, grads, grads_t, gates, gates_t)
+    mix, back, out = pl.pallas_call(
+        functools.partial(expert_kernel, first_expert, min(256, row_count), feat_tile),
+        grid=(count,),
+        in_specs=[whole(a) for a in fixed] + [block, whole(mix), whole(back)],
+        out_specs=[whole(mix), whole(back), out_block],
+        out_shape=[
+            jax.ShapeDtypeStruct(mix.shape, mix.dtype),
+            jax.ShapeDtypeStruct(back.shape, back.dtype),
+            jax.ShapeDtypeStruct((groups, kinds, count, inner, hidden), jnp.bfloat16),
+        ],
+        scratch_shapes=[
+            pltpu.VMEM((row_count, hidden), jnp.bfloat16),
+            pltpu.VMEM((row_count, 2 * hidden), jnp.bfloat16),
+        ],
+        input_output_aliases={7: 0, 8: 1},
+        cost_estimate=pl.CostEstimate(
+            flops=18 * count * row_count * width * hidden,
+            bytes_accessed=4 * count * kinds * width * hidden + 16 * mix.size,
+            transcendentals=count * row_count * hidden,
+        ),
+        name="expert_pass",
+    )(*fixed, weights, mix, back)
+    if packed:
+        out = out.reshape(kinds, count, shards, depth, hidden).transpose(2, 0, 1, 3, 4)
+    return (mix, back, out)
+
+
+def swap(part):
+    count = lax.axis_size("tensor")
+    return lax.ppermute(part, "tensor", [(i, (i + 1) % count) for i in range(count)])
+
+
+def both_halves(mine):
+    other = swap(mine)
+    first = lax.axis_index("tensor") == 0
+    return jnp.concatenate(
+        [jnp.where(first, mine, other), jnp.where(first, other, mine)], axis=0
+    )
+
+
+def sum_halves(part):
+    half = part.shape[0] // 2
+    place = lax.axis_index("tensor")
+    mine = lax.dynamic_slice_in_dim(part, place * half, half, 0)
+    given = lax.dynamic_slice_in_dim(part, (1 - place) * half, half, 0).astype(jnp.bfloat16)
+    return mine.astype(jnp.bfloat16).astype(jnp.float32) + swap(given).astype(jnp.float32)
+
+
+def scatter_sum(parts):
+    place = lax.axis_index("dp")
+    count = parts.shape[0]
+    size = count
+    bit = 1
+    total = parts
+    while size > 1:
+        pairs = total.reshape((size // 2, 2) + parts.shape[1:])
+        mine = (place // bit) % 2
+        keep = lax.dynamic_index_in_dim(pairs, mine, 1, keepdims=False)
+        give = lax.dynamic_index_in_dim(pairs, 1 - mine, 1, keepdims=False)
+        taken = lax.ppermute(give, "dp", [(i, i ^ bit) for i in range(count)])
+        total = keep.astype(jnp.float32) + taken.astype(jnp.float32)
+        size //= 2
+        bit *= 2
+        if size > 1:
+            total = total.astype(jnp.bfloat16)
+    return total.reshape(parts.shape[1:])
+
+
+def sum_everywhere(value):
+    for axis in ("tensor", "dp"):
+        count = lax.axis_size(axis)
+        bit = 1
+        while bit < count:
+            value = value + lax.ppermute(value, axis, [(i, i ^ bit) for i in range(count)])
+            bit *= 2
+    return value
 
 
 def local(
@@ -259,67 +351,74 @@
     gate_weights,
     seq_lengths,
 ):
-    gathered = (
-        lax.all_gather(query_weight, "dp", axis=0, tiled=True),
-        lax.all_gather(key_weight, "dp", axis=0, tiled=True),
-        lax.all_gather(value_weight, "dp", axis=0, tiled=True),
-        lax.all_gather(output_weight, "dp", axis=0, tiled=True),
-        lax.all_gather(gate_weight, "dp", axis=1, tiled=True),
-        lax.all_gather(up_weight, "dp", axis=1, tiled=True),
-        lax.all_gather(down_weight, "dp", axis=1, tiled=True),
-    )
-    query_full, key_full, value_full, output_full, gate_full, up_full, down_full = gathered
+    expert_count = gate_weight.shape[0]
+    heads_cols = query_weight.shape[1]
+    kv_cols = key_weight.shape[1]
+    qkv_cols = heads_cols + 2 * kv_cols
+    dense_mine = jnp.concatenate([query_weight, key_weight, value_weight, output_weight], axis=1)
+    dense_full = lax.all_gather(dense_mine, "dp", axis=0, tiled=True)
+    qkv_full, output_full = dense_full[:, :qkv_cols], dense_full[:, qkv_cols:]
+    stacked = (gate_weight, up_weight, down_weight)
+    held = expert_count // GATHERS
+    gathered = [
+        lax.all_gather(jnp.stack([w[i * held : (i + 1) * held] for w in stacked]), "dp")
+        for i in range(GATHERS)
+    ]
+
     row_count = expert_ids.shape[0]
     doc_ids, positions, live_rows = row_layout(seq_lengths[0], row_count)
     cosine, sine_table = rope_tables(positions, HEAD_DIM)
+    both = both_halves(jnp.concatenate([tokens, out_grad], axis=1))
+    tokens_all, grad_all = both[:, : tokens.shape[1]], both[:, tokens.shape[1] :]
     widened = tokens.astype(jnp.float32)
     unit_attn, inv_attn = rms_rows(widened)
-    normed = (unit_attn * attn_norm).astype(jnp.bfloat16)
-    normed_all = lax.all_gather(normed, "tensor", axis=0, tiled=True)
-    head_count = query_full.shape[1] // HEAD_DIM
-    kv_count = key_full.shape[1] // HEAD_DIM
-    queries = rotate(
-        plain_dot(normed_all, query_full).reshape(row_count, head_count, HEAD_DIM),
+    unit_all, _ = rms_rows(tokens_all.astype(jnp.float32))
+    normed_all = (unit_all * attn_norm).astype(jnp.bfloat16)
+    head_count = heads_cols // HEAD_DIM
+    kv_count = kv_cols // HEAD_DIM
+    qkv = plain_dot(normed_all, qkv_full)
+    turned = rotate(
+        qkv[:, : heads_cols + kv_cols].reshape(row_count, head_count + kv_count, HEAD_DIM),
         cosine,
         sine_table,
     ).astype(jnp.bfloat16)
-    keys_rot = rotate(
-        plain_dot(normed_all, key_full).reshape(row_count, kv_count, HEAD_DIM), cosine, sine_table
-    ).astype(jnp.bfloat16)
+    queries, keys_rot = turned[:, :head_count], turned[:, head_count:]
     values = (
-        plain_dot(normed_all, value_full)
+        qkv[:, heads_cols + kv_cols :]
         .astype(jnp.bfloat16)
         .reshape(row_count, kv_count, HEAD_DIM)
     )
     attn_rows, log_totals = attend(queries, keys_rot, values, doc_ids, live_rows)
     attn_flat = attn_rows.reshape(row_count, head_count * HEAD_DIM)
-    after_attn = widened + lax.psum_scatter(
-        times_t(attn_flat, output_full).astype(jnp.bfloat16),
-        "tensor",
-        scatter_dimension=0,
-        tiled=True,
-    ).astype(jnp.float32)
+    after_attn = widened + sum_halves(times_t(attn_flat, output_full))
     unit_moe, inv_moe = rms_rows(after_attn)
     expert_in = (unit_moe * moe_norm).astype(jnp.bfloat16)
-    expert_all = lax.all_gather(expert_in, "tensor", axis=0, tiled=True)
-    sources, slot_gate = slot_map(expert_ids, live_rows, gate_weights, gate_full.shape[0], CAP)
-    mix_part, kept = expert_forward(expert_all, sources, slot_gate, gate_full, up_full, down_full)
-    mixed = lax.psum_scatter(
-        mix_part.astype(jnp.bfloat16), "tensor", scatter_dimension=0, tiled=True
-    ).astype(jnp.float32)
-    block_out = (after_attn + mixed).astype(jnp.bfloat16)
-    grad_all = lax.all_gather(out_grad, "tensor", axis=0, tiled=True)
-    moe_part, expert_grads = expert_backward(
-        expert_all, grad_all, sources, slot_gate, gate_full, up_full, down_full, kept
-    )
-    moe_grad = lax.psum_scatter(
-        moe_part.astype(jnp.bfloat16), "tensor", scatter_dimension=0, tiled=True
-    ).astype(jnp.float32)
+    expert_all = both_halves(expert_in)
+
+    gates = expert_gates(expert_ids, gate_weights, live_rows, expert_count)
+    fixed = (expert_all, expert_all.T, grad_all, grad_all.T, gates, gates.T)
+    mix_part = jnp.zeros(expert_all.shape, jnp.float32)
+    moe_part = jnp.zeros(expert_all.shape, jnp.float32)
+    summed_experts = []
+    count = expert_count // PASSES
+    for low in range(0, expert_count, count):
+        weights, offset = gathered[low // held], low % held
+        mix_part, moe_part, grads = expert_pass(
+            low, count, offset, *fixed, weights, mix_part, moe_part
+        )
+        summed_experts.append(scatter_sum(grads))
+
+    moe_grad = sum_halves(moe_part)
     back_moe, grad_moe_norm = norm_back(moe_grad, unit_moe, inv_moe, moe_norm)
     resid_grad = out_grad.astype(jnp.float32) + back_moe
-    resid_half = resid_grad.astype(jnp.bfloat16)
-    resid_all = lax.all_gather(resid_half, "tensor", axis=0, tiled=True)
-    grad_output = inner_rows(resid_all, attn_flat)
+    resid_all = both_halves(resid_grad.astype(jnp.bfloat16))
+    mixed = sum_halves(mix_part)
+    block_out = (after_attn + mixed).astype(jnp.bfloat16)
+    output_sum = scatter_sum(
+        inner_rows(resid_all, attn_flat)
+        .astype(jnp.bfloat16)
+        .reshape(lax.axis_size("dp"), -1, heads_cols),
+    )
     attn_grad = (
         plain_dot(resid_all, output_full)
         .astype(jnp.bfloat16)
@@ -333,43 +432,28 @@
     )
     key_pre = rotate_back(key_grad, cosine, sine_table).astype(jnp.bfloat16).reshape(row_count, -1)
     value_pre = value_grad.astype(jnp.bfloat16).reshape(row_count, -1)
-    grad_query = inner_rows(normed_all, query_pre)
-    grad_key = inner_rows(normed_all, key_pre)
-    grad_value = inner_rows(normed_all, value_pre)
-    attn_in_grad = lax.psum_scatter(
-        (
-            times_t(query_pre, query_full)
-            + times_t(key_pre, key_full)
-            + times_t(value_pre, value_full)
-        ).astype(jnp.bfloat16),
-        "tensor",
-        scatter_dimension=0,
-        tiled=True,
-    ).astype(jnp.float32)
+    pre_all = jnp.concatenate([query_pre, key_pre, value_pre], axis=1)
+    shards = lax.axis_size("dp")
+    qkv_sum = scatter_sum(
+        inner_rows(normed_all, pre_all).astype(jnp.bfloat16).reshape(shards, -1, qkv_cols),
+    )
+    attn_in_grad = sum_halves(times_t(pre_all, qkv_full))
     back_attn, grad_attn_norm = norm_back(attn_in_grad, unit_attn, inv_attn, attn_norm)
     input_grad = resid_grad + back_attn
-    gain_sums = lax.psum((grad_attn_norm, grad_moe_norm), ("dp", "tensor"))
-    summed = (
-        lax.psum_scatter(grad_query, "dp", scatter_dimension=0, tiled=True),
-        lax.psum_scatter(grad_key, "dp", scatter_dimension=0, tiled=True),
-        lax.psum_scatter(grad_value, "dp", scatter_dimension=0, tiled=True),
-        lax.psum_scatter(grad_output, "dp", scatter_dimension=0, tiled=True),
-        lax.psum_scatter(expert_grads[0], "dp", scatter_dimension=1, tiled=True),
-        lax.psum_scatter(expert_grads[1], "dp", scatter_dimension=1, tiled=True),
-        lax.psum_scatter(expert_grads[2], "dp", scatter_dimension=1, tiled=True),
-    )
+    gain_sums = sum_everywhere(jnp.stack([grad_attn_norm, grad_moe_norm]))
+    expert_sum = jnp.concatenate(summed_experts, axis=1)
     return (
         block_out,
         input_grad,
         gain_sums[0],
-        summed[0],
-        summed[1],
-        summed[2],
-        summed[3],
+        qkv_sum[:, :heads_cols],
+        qkv_sum[:, heads_cols : heads_cols + kv_cols],
+        qkv_sum[:, heads_cols + kv_cols :],
+        output_sum,
         gain_sums[1],
-        summed[4],
-        summed[5],
-        summed[6],
+        expert_sum[0],
+        expert_sum[1],
+        expert_sum[2],
     )
 
 
@@ -403,4 +487,5 @@
         P(None, "dp", "tensor"),
         P(None, "dp", "tensor"),
     )
+
     return jax.shard_map(local, mesh=mesh, in_specs=in_specs, out_specs=out_specs, check_vma=False)

time: 2760 us -> 988 us (0.36)
  waiting for transfers between devices: 1650 us -> 584 us
  matrix products: 454 us -> 44.6 us
  other arithmetic: 334 us -> 103 us
  Pallas kernels: 0 us -> 113 us
  local copies, waits for them, and re-layouts: 187 us -> 83.7 us
  blocking collectives: 85.6 us -> 0 us
    reduce_scatter x11 -> x0, waiting for transfers between devices: 1190 us -> none  [the longest x1 295 us: local(): lax.psum_scatter(expert_grads[0], 'dp', scatter_dimension=1, tiled=True)]
    ppermute x0 -> x36, waiting for transfers between devices: none -> 461 us  [the longest x24 352 us: scatter_sum(): taken = lax.ppermute(give, 'dp', [(i, i ^ bit) for i in range(count)])]
    all_gather x9 -> x3, waiting for transfers between devices: 450 us -> 123 us  [the longest x2 104 us: local(): lax.all_gather(jnp.stack([w[i * held:(i + 1) * held] for w in stacked]),...]
    scatter-add x40 -> x0, other arithmetic: 297 us -> none  [the longest x20 149 us: one_expert(): accum = accum.at[source_e].add(result * gate_e[:, None])]
    dot_general x64 -> x2, matrix products: 146 us -> 8.01 us  [times_t(): lax.dot_general(first_op, weight, (((1,), (1,)), ((), ())), preferred_ele...]
    dot_general x64 -> x2, matrix products: 144 us -> 8.55 us  [plain_dot(): return jnp.dot(first_op, weight, preferred_element_type=jnp.float32)]
    dot_general x64 -> x2, matrix products: 138 us -> 3.69 us  [inner_rows(): lax.dot_general(first_op, second_op, (((0,), (0,)), ((), ())), preferred_...]
    gather x60 -> x0, local copies, waits for them, and re-layouts: 129 us -> none  [the longest x40 86.5 us: one_expert(): rows_e = padded_rows[source_e]]
  transfers between devices with their start and end apart: 20 -> 39, of which waited for: 17 -> 25; matrix products, arithmetic and copies ran while one was open for 3% -> 16% of each run, Pallas kernels for 0% -> 6%
where the time goes in v1:
time: 988 us; the launch traced here: 983 us
  waiting for transfers between devices  584 us (59%)
  Pallas kernels  113 us (11%)
  other arithmetic  103 us (10%)
  local copies, waits for them, and re-layouts  83.7 us (8%)
  matrix products  44.6 us (5%)
  starting transfers between devices  38.6 us (4%)
  between operations  15.5 us (2%)
    ppermute x24, waiting for transfers between devices, scatter_sum(): taken = lax.ppermute(give, 'dp', [(i, i ^ bit) for i in range(count)])  352 us
    pallas_call x4, Pallas kernels, expert_pass(): pl.pallas_call(functools.partial(expert_kernel, first_expert, min(256, ro...  113 us
    all_gather x2, waiting for transfers between devices, local(): lax.all_gather(jnp.stack([w[i * held:(i + 1) * held] for w in stacked]),...  104 us
    ppermute x7, waiting for transfers between devices, swap(): lax.ppermute(part, 'tensor', [(i, (i + 1) % count) for i in range(count)])  96.6 us
    convert_element_type x18, other arithmetic, scatter_sum(): total = total.astype(jnp.bfloat16)  52 us
    squeeze x24, local copies, waits for them, and re-layouts, scatter_sum(): give = lax.dynamic_index_in_dim(pairs, 1 - mine, 1, keepdims=False)  27.2 us
    dot_general x6, matrix products, batched(): jnp.einsum(pattern, first_op, second_op, preferred_element_type=jnp.float32)  24.3 us
    ppermute x24, starting transfers between devices, scatter_sum(): taken = lax.ppermute(give, 'dp', [(i, i ^ bit) for i in range(count)])  19.9 us
  transfers between devices with their start and end apart: 39, of which 25 were waited for; matrix products, arithmetic and copies ran while one was open for 16% of the time, Pallas kernels for 6%

profile of v1, /device:TPU:0, one launch (start us, length us, event | category | flops | bytes accessed | tf_op | source)
XLA Modules:
  0.0 982.6 jit_solution(12723264718294724486)
XLA Ops:
  14.9 3.1 collective-permute-start
  20.3 32.1 %collective-permute-done = bf16[256,3072]{0,1:T(8,128)(2,1)} collective-permute-done((bf16[256,3072]{0,1:T(8,128)(2,1)S(1)}, bf16[256,3072]{0,1:T(8,128)(2,1)}, u32[]{:S(2)}, u32[]{:S(2)}) %collective-permute-start) | collective-permute-done | bytes 1572896 | tf_op jit(solution)/shard_map/ppermute | solution.py:289
  56.1 18.9 %all-gather.6.cloned.1.call-done = bf16[1536,2048]{1,0:T(8,128)(2,1)} async-done(((bf16[96,2048]{1,0:T(8,128)(2,1)}), bf16[1536,2048]{1,0:T(8,128)(2,1)}) %all-gather.6.cloned.1.call-update) | async-done | bytes 6291472 | tf_op jit(solution)/shard_map/all_gather | solution.py:359
  75.0 4.6 fusion.18
  81.2 3.5 copy.204
  92.4 2.6 fusion.4
  96.9 3.6 fusion.52
  100.6 3.4 fusion.35
  107.0 18.0 %collective-permute-done.1 = bf16[256,1536]{0,1:T(8,128)(2,1)} collective-permute-done((bf16[256,1536]{0,1:T(8,128)(2,1)S(1)}, bf16[256,1536]{0,1:T(8,128)(2,1)}, u32[]{:S(2)}, u32[]{:S(2)}) %collective-permute-start.1) | collective-permute-done | bytes 786464 | tf_op jit(solution)/shard_map/ppermute | solution.py:289
  125.0 2.4 multiply_reduce_fusion.3
  131.3 2.6 pad_maximum_fusion.1
  133.9 2.6 copy.218.grads_ref
  136.5 11.2 %collective-permute-done.2 = bf16[256,1536]{0,1:T(8,128)(2,1)} collective-permute-done((bf16[256,1536]{0,1:T(8,128)(2,1)}, bf16[256,1536]{0,1:T(8,128)(2,1)}, u32[]{:S(2)}, u32[]{:S(2)}) %collective-permute-start.2) | collective-permute-done | bytes 786464 | tf_op jit(solution)/shard_map/ppermute | solution.py:289
  151.3 2.6 copy.217.rows_ref
  153.8 42.6 %all-gather.10.cloned.1.call-done = bf16[48,10,96,256]{3,2,1,0:T(8,128)(2,1)} async-done(((bf16[3,10,96,256]{3,2,1,0:T(8,128)(2,1)}), bf16[48,10,96,256]{3,2,1,0:T(8,128)(2,1)}) %all-gather.10.cloned.1.call-update) | async-done | bytes 23592976 | tf_op jit(solution)/shard_map/all_gather | solution.py:364
  200.6 29.1 %expert_pass.4 = (f32[512,1536]{1,0:T(8,128)}, f32[512,1536]{1,0:T(8,128)}, bf16[16,3,5,96,256]{4,3,2,1,0:T(8,128)(2,1)}) custom-call(bf16[512,1536]{1,0:T(8,128)(2,1)} %copy.217.rows_ref, bf16[1536,512]{1,0:T(8,128)(2,1)} %get-tuple-element.177.rows_t_ref, bf16[512,1536]{1,0:T(8,128)(2,1)} %copy.218.grads_ref, ...), custom_call_target="tpu_custom_call", output_to_operand_aliasing={{0}: (7, {}), {1}: (8, {})} | custom-call | flops 18119393280 | bytes 36175872 | tf_op jit(solution)/shard_map/expert_pass/pallas_call | solution.py:260
  229.7 28.3 %expert_pass.5 = (f32[512,1536]{1,0:T(8,128)}, f32[512,1536]{1,0:T(8,128)}, bf16[16,3,5,96,256]{4,3,2,1,0:T(8,128)(2,1)}) custom-call(bf16[512,1536]{1,0:T(8,128)(2,1)} %copy.217.rows_ref, bf16[1536,512]{1,0:T(8,128)(2,1)} %get-tuple-element.177.rows_t_ref, bf16[512,1536]{1,0:T(8,128)(2,1)} %copy.218.grads_ref, ...), custom_call_target="tpu_custom_call", output_to_operand_aliasing={{0}: (7, {}), {1}: (8, {})} | custom-call | flops 18119393280 | bytes 36175872 | tf_op jit(solution)/shard_map/expert_pass/pallas_call | solution.py:260
  257.9 61.3 %all-gather.8.cloned.1.call-done = bf16[48,10,96,256]{3,2,1,0:T(8,128)(2,1)} async-done(((bf16[3,10,96,256]{3,2,1,0:T(8,128)(2,1)}), bf16[48,10,96,256]{3,2,1,0:T(8,128)(2,1)}) %all-gather.8.cloned.1.call-update) | async-done | bytes 23592976 | tf_op jit(solution)/shard_map/all_gather | solution.py:364
  319.2 28.2 %expert_pass.6 = (f32[512,1536]{1,0:T(8,128)}, f32[512,1536]{1,0:T(8,128)}, bf16[16,3,5,96,256]{4,3,2,1,0:T(8,128)(2,1)}) custom-call(bf16[512,1536]{1,0:T(8,128)(2,1)} %copy.217.rows_ref, bf16[1536,512]{1,0:T(8,128)(2,1)} %get-tuple-element.177.rows_t_ref, bf16[512,1536]{1,0:T(8,128)(2,1)} %copy.218.grads_ref, ...), custom_call_target="tpu_custom_call", output_to_operand_aliasing={{0}: (7, {}), {1}: (8, {})} | custom-call | flops 18119393280 | bytes 36175872 | tf_op jit(solution)/shard_map/expert_pass/pallas_call | solution.py:260
  347.4 27.9 %expert_pass.7 = (f32[512,1536]{1,0:T(8,128)}, f32[512,1536]{1,0:T(8,128)}, bf16[16,3,5,96,256]{4,3,2,1,0:T(8,128)(2,1)}) custom-call(bf16[512,1536]{1,0:T(8,128)(2,1)} %copy.217.rows_ref, bf16[1536,512]{1,0:T(8,128)(2,1)} %get-tuple-element.177.rows_t_ref, bf16[512,1536]{1,0:T(8,128)(2,1)} %copy.218.grads_ref, ...), custom_call_target="tpu_custom_call", output_to_operand_aliasing={{0}: (7, {}), {1}: (8, {})} | custom-call | flops 18119393280 | bytes 36175872 | tf_op jit(solution)/shard_map/expert_pass/pallas_call | solution.py:260
  375.3 3.4 copy.223
  381.6 18.2 %collective-permute-done.4 = bf16[256,1536]{0,1:T(8,128)(2,1)S(1)} collective-permute-done((bf16[256,1536]{0,1:T(8,128)(2,1)S(1)}, bf16[256,1536]{0,1:T(8,128)(2,1)S(1)}, u32[]{:S(2)}, u32[]{:S(2)}) %collective-permute-start.4) | collective-permute-done | bytes 786464 | tf_op jit(solution)/shard_map/ppermute | solution.py:289
  404.7 17.1 %collective-permute-done.5 = bf16[256,1536]{0,1:T(8,128)(2,1)} collective-permute-done((bf16[256,1536]{0,1:T(8,128)(2,1)}, bf16[256,1536]{0,1:T(8,128)(2,1)}, u32[]{:S(2)}, u32[]{:S(2)}) %collective-permute-start.5) | collective-permute-done | bytes 786464 | tf_op jit(solution)/shard_map/ppermute | solution.py:289
  424.4 4.0 fusion.49
  432.3 9.2 multiply_convert_fusion
  443.8 3.2 convolution_multiply_fusion
  448.1 4.1 fusion.7
  453.5 2.5 reduce_sum.147
  459.0 2.3 reduce_sum.148
  461.3 2.4 fusion.46
  463.8 4.6 fusion.16
  472.0 5.7 dynamic-slice_bitcast_fusion.3
  477.7 2.9 dynamic-slice_bitcast_fusion.2
  481.1 3.0 copy.220
  486.8 5.7 dynamic-slice_bitcast_fusion.1
  492.6 2.7 fusion.42
  498.3 7.9 collective-permute-done.7
  515.9 2.5 collective-permute-start.11
  521.9 3.0 dynamic-slice_bitcast_fusion
  524.9 9.8 collective-permute-done.17
  539.3 2.7 fusion.15
  543.1 4.1 collective-permute-done.18
  548.4 3.9 fusion.41
  552.3 3.1 copy.242
  557.7 13.1 %collective-permute-done.13 = bf16[4,96,1280]{2,1,0:T(8,128)(2,1)} collective-permute-done((bf16[4,96,1280]{2,1,0:T(8,128)(2,1)}, bf16[4,96,1280]{2,1,0:T(8,128)(2,1)}, u32[]{:S(2)}, u32[]{:S(2)}) %collective-permute-start.13) | collective-permute-done | bytes 983072 | tf_op jit(solution)/shard_map/ppermute | solution.py:319
  570.8 2.4 collective-permute-start.19
  576.4 6.9 fusion.3
  587.2 6.9 fusion.2
  598.9 6.9 fusion.1
  609.8 7.1 fusion
  620.8 9.2 collective-permute-done.15
  630.9 22.8 %collective-permute-done.21 = bf16[4,3,5,96,256]{4,3,2,1,0:T(8,128)(2,1)} collective-permute-done((bf16[4,3,5,96,256]{4,3,2,1,0:T(8,128)(2,1)}, bf16[4,3,5,96,256]{4,3,2,1,0:T(8,128)(2,1)}, u32[]{:S(2)}, u32[]{:S(2)}) %collective-permute-start.21) | collective-permute-done | bytes 2949152 | tf_op jit(solution)/shard_map/ppermute | solution.py:319
  653.7 3.8 fusion.14
  658.2 58.7 %collective-permute-done.25 = bf16[4,3,5,96,256]{4,3,2,1,0:T(8,128)(2,1)} collective-permute-done((bf16[4,3,5,96,256]{4,3,2,1,0:T(8,128)(2,1)}, bf16[4,3,5,96,256]{4,3,2,1,0:T(8,128)(2,1)}, u32[]{:S(2)}, u32[]{:S(2)}) %collective-permute-start.25) | collective-permute-done | bytes 2949152 | tf_op jit(solution)/shard_map/ppermute | solution.py:319
  716.9 3.0 fusion.13
  720.5 59.6 %collective-permute-done.29 = bf16[4,3,5,96,256]{4,3,2,1,0:T(8,128)(2,1)} collective-permute-done((bf16[4,3,5,96,256]{4,3,2,1,0:T(8,128)(2,1)}, bf16[4,3,5,96,256]{4,3,2,1,0:T(8,128)(2,1)}, u32[]{:S(2)}, u32[]{:S(2)}) %collective-permute-start.29) | collective-permute-done | bytes 2949152 | tf_op jit(solution)/shard_map/ppermute | solution.py:319
  780.1 3.0 fusion.12
  783.7 56.8 %collective-permute-done.33 = bf16[4,3,5,96,256]{4,3,2,1,0:T(8,128)(2,1)S(1)} collective-permute-done((bf16[4,3,5,96,256]{4,3,2,1,0:T(8,128)(2,1)S(1)}, bf16[4,3,5,96,256]{4,3,2,1,0:T(8,128)(2,1)S(1)}, u32[]{:S(2)}, u32[]{:S(2)}) %collective-permute-start.33) | collective-permute-done | bytes 2949152 | tf_op jit(solution)/shard_map/ppermute | solution.py:319
  847.4 2.5 collective-permute-start.27
  852.4 48.6 %collective-permute-done.34 = bf16[2,3,5,96,256]{4,3,2,1,0:T(8,128)(2,1)S(1)} collective-permute-done((bf16[2,3,5,96,256]{4,3,2,1,0:T(8,128)(2,1)S(1)}, bf16[2,3,5,96,256]{4,3,2,1,0:T(8,128)(2,1)S(1)}, u32[]{:S(2)}, u32[]{:S(2)}) %collective-permute-start.34) | collective-permute-done | bytes 1474592 | tf_op jit(solution)/shard_map/ppermute | solution.py:319
  902.0 42.2 %collective-permute-done.27 = bf16[1,3,5,96,256]{4,3,2,1,0:T(8,128)(2,1)S(1)} collective-permute-done((bf16[1,3,5,96,256]{4,3,2,1,0:T(8,128)(2,1)S(1)}, bf16[1,3,5,96,256]{4,3,2,1,0:T(8,128)(2,1)S(1)}, u32[]{:S(2)}, u32[]{:S(2)}) %collective-permute-start.27) | collective-permute-done | bytes 737312 | tf_op jit(solution)/shard_map/ppermute | solution.py:319
  944.4 15.6 %collective-permute-done.31 = bf16[1,3,5,96,256]{4,3,2,1,0:T(8,128)(2,1)S(1)} collective-permute-done((bf16[1,3,5,96,256]{4,3,2,1,0:T(8,128)(2,1)S(1)}, bf16[1,3,5,96,256]{4,3,2,1,0:T(8,128)(2,1)S(1)}, u32[]{:S(2)}, u32[]{:S(2)}) %collective-permute-start.31) | collective-permute-done | bytes 737312 | tf_op jit(solution)/shard_map/ppermute | solution.py:319
  960.2 11.8 %collective-permute-done.35 = bf16[1,3,5,96,256]{4,3,2,1,0:T(8,128)(2,1)S(1)} collective-permute-done((bf16[1,3,5,96,256]{4,3,2,1,0:T(8,128)(2,1)S(1)}, bf16[1,3,5,96,256]{4,3,2,1,0:T(8,128)(2,1)S(1)}, u32[]{:S(2)}, u32[]{:S(2)}) %collective-permute-start.35) | collective-permute-done | bytes 737312 | tf_op jit(solution)/shard_map/ppermute | solution.py:319
  972.9 2.8 slice_bitcast_fusion
  (332 shorter events, 126.9 us)
Async XLA Ops:
  7.2 67.8 %all-gather.6.cloned.1.call-start = ((), (), s32[]{:S(2)}) async-start(), calls=%async_computation | async-start | bytes 6684672 | tf_op jit(solution)/shard_map/all_gather | solution.py:359
  9.2 187.3 %all-gather.10.cloned.1.call-start = ((), (), s32[]{:S(2)}) async-start(), calls=%async_computation.2 | async-start | bytes 25067520 | tf_op jit(solution)/shard_map/all_gather | solution.py:364
  12.0 307.2 %all-gather.8.cloned.1.call-start = ((), (), s32[]{:S(2)}) async-start(), calls=%async_computation.1 | async-start | bytes 25067520 | tf_op jit(solution)/shard_map/all_gather | solution.py:364
  14.9 37.6 %collective-permute-start = (bf16[256,3072]{0,1:T(8,128)(2,1)S(1)}, bf16[256,3072]{0,1:T(8,128)(2,1)}, u32[]{:S(2)}, u32[]{:S(2)}) collective-permute-start(bf16[256,3072]{0,1:T(8,128)(2,1)S(1)} %pad_maximum_fusion.2), channel_id=1, source_target_pairs={{0,1},{1,0},{2,3},{3,2},{4,5},{5,4},{6,7},{7,6},{8,9},{9,8},{10,11... | collective-permute-start | bytes 4718600 | tf_op jit(solution)/shard_map/ppermute | solution.py:289
  19.3 67.4 %copy-start.24 = (f32[512,64]{0,1:T(8,128)}, f32[512,64]{0,1:T(8,128)S(1)}, u32[]{:S(2)}) copy-start(f32[512,64]{0,1:T(8,128)S(1)} %get-tuple-element.200) | copy-start | bytes 393220
  19.3 67.4 %copy-start.33 = (f32[512,64]{0,1:T(8,128)}, f32[512,64]{0,1:T(8,128)S(1)}, u32[]{:S(2)}) copy-start(f32[512,64]{0,1:T(8,128)S(1)} %get-tuple-element.193) | copy-start | bytes 393220
  54.5 20.6 %copy-start.59 = (f32[1536]{0:T(1024)S(1)}, f32[1536]{0:T(1024)}, u32[]{:S(2)}) copy-start(f32[1536]{0:T(1024)} %param.16) | copy-start | bytes 18436
  56.1 23.5 %copy-start.30 = (bf16[512,1536]{0,1:T(8,128)(2,1)}, bf16[512,1536]{0,1:T(8,128)(2,1)S(1)}, u32[]{:S(2)}) copy-start(bf16[512,1536]{0,1:T(8,128)(2,1)S(1)} %get-tuple-element.163) | copy-start | bytes 4718596
  56.1 23.5 %copy-start.66 = (f32[512]{0:T(512)}, f32[512]{0:T(512)S(1)}, u32[]{:S(2)}) copy-start(f32[512]{0:T(512)S(1)} %add_rsqrt_fusion) | copy-start | bytes 6148
  105.2 22.3 %copy-start.57 = (f32[1536]{0:T(1024)S(1)}, f32[1536]{0:T(1024)}, u32[]{:S(2)}) copy-start(f32[1536]{0:T(1024)} %param.21) | copy-start | bytes 18436
  105.2 19.8 %collective-permute-start.1 = (bf16[256,1536]{0,1:T(8,128)(2,1)S(1)}, bf16[256,1536]{0,1:T(8,128)(2,1)}, u32[]{:S(2)}, u32[]{:S(2)}) collective-permute-start(bf16[256,1536]{0,1:T(8,128)(2,1)S(1)} %dynamic-slice_convert_fusion.6), channel_id=1, source_target_pairs={{0,1},{1,0},{2,3},{3,2},{4,5},{5,4},{6,7},{7,6},{8,9},{9,8},{10,11... | collective-permute-start | bytes 2359304 | tf_op jit(solution)/shard_map/ppermute | solution.py:289
  128.6 19.1 %collective-permute-start.2 = (bf16[256,1536]{0,1:T(8,128)(2,1)}, bf16[256,1536]{0,1:T(8,128)(2,1)}, u32[]{:S(2)}, u32[]{:S(2)}) collective-permute-start(bf16[256,1536]{0,1:T(8,128)(2,1)} %multiply_convert_fusion.1), channel_id=1, source_target_pairs={{0,1},{1,0},{2,3},{3,2},{4,5},{5,4},{6,7},{7,6},{8,9},{9,8},{10,11... | collective-permute-start | bytes 2359304 | tf_op jit(solution)/shard_map/ppermute | solution.py:289
  378.7 21.1 %copy-start.14 = (bf16[512,1536]{0,1:T(8,128)(2,1)S(1)}, bf16[512,1536]{0,1:T(8,128)(2,1)}, u32[]{:S(2)}) copy-start(bf16[512,1536]{0,1:T(8,128)(2,1)} %copy.223) | copy-start | bytes 4718596
  380.1 19.8 %collective-permute-start.4 = (bf16[256,1536]{0,1:T(8,128)(2,1)S(1)}, bf16[256,1536]{0,1:T(8,128)(2,1)S(1)}, u32[]{:S(2)}, u32[]{:S(2)}) collective-permute-start(bf16[256,1536]{0,1:T(8,128)(2,1)S(1)} %dynamic-slice_convert_fusion.2), channel_id=1, source_target_pairs={{0,1},{1,0},{2,3},{3,2},{4,5},{5,4},{6,7},{7,6},{8,9},{9,8},{10,11... | collective-permute-start | bytes 2359304 | tf_op jit(solution)/shard_map/ppermute | solution.py:289
  402.6 19.2 %collective-permute-start.5 = (bf16[256,1536]{0,1:T(8,128)(2,1)}, bf16[256,1536]{0,1:T(8,128)(2,1)}, u32[]{:S(2)}, u32[]{:S(2)}) collective-permute-start(bf16[256,1536]{0,1:T(8,128)(2,1)} %fusion.78), channel_id=1, source_target_pairs={{0,1},{1,0},{2,3},{3,2},{4,5},{5,4},{6,7},{7,6},{8,9},{9,8},{10,11... | collective-permute-start | bytes 2359304 | tf_op jit(solution)/shard_map/ppermute | solution.py:289
  432.3 9.2 copy-start.20
  463.7 14.0 %slice-start.10 = ((s8[11796480]{0:T(1024)(128)(4,1)}), s8[4194304]{0:T(1024)(128)(4,1)S(1)}, s32[]{:S(2)}) async-start(s8[11796480]{0:T(1024)(128)(4,1)} %bitcast.239), calls=%async_computation.13 | async-start | bytes 8388608
  463.8 14.0 %slice-start.11 = ((s8[11796480]{0:T(1024)(128)(4,1)}), s8[4194304]{0:T(1024)(128)(4,1)S(1)}, s32[]{:S(2)}) async-start(s8[11796480]{0:T(1024)(128)(4,1)} %bitcast.239), calls=%async_computation.14 | async-start | bytes 8388608
  470.5 22.1 %collective-permute-start.6 = (bf16[256,1536]{0,1:T(8,128)(2,1)}, bf16[256,1536]{0,1:T(8,128)(2,1)}, u32[]{:S(2)}, u32[]{:S(2)}) collective-permute-start(bf16[256,1536]{0,1:T(8,128)(2,1)} %dynamic-slice_convert_fusion), channel_id=1, source_target_pairs={{0,1},{1,0},{2,3},{3,2},{4,5},{5,4},{6,7},{7,6},{8,9},{9,8},{10,11... | collective-permute-start | bytes 2359304 | tf_op jit(solution)/shard_map/ppermute | solution.py:289
  477.7 97.0 %collective-permute-start.20 = (bf16[8,3,5,96,256]{4,3,2,1,0:T(8,128)(2,1)}, bf16[8,3,5,96,256]{4,3,2,1,0:T(8,128)(2,1)}, u32[]{:S(2)}, u32[]{:S(2)}) collective-permute-start(bf16[8,3,5,96,256]{4,3,2,1,0:T(8,128)(2,1)} %dynamic-slice_bitcast_fusion.3), channel_id=1, source_target_pairs={{0,2},{2,0},{4,6},{6,4},{8,10},{10,8},{12,14},{14,12},{16,18},{18,... | collective-permute-start | bytes 17694728 | tf_op jit(solution)/shard_map/ppermute | solution.py:319
  480.6 106.0 %collective-permute-start.24 = (bf16[8,3,5,96,256]{4,3,2,1,0:T(8,128)(2,1)}, bf16[8,3,5,96,256]{4,3,2,1,0:T(8,128)(2,1)}, u32[]{:S(2)}, u32[]{:S(2)}) collective-permute-start(bf16[8,3,5,96,256]{4,3,2,1,0:T(8,128)(2,1)} %dynamic-slice_bitcast_fusion.2), channel_id=1, source_target_pairs={{0,2},{2,0},{4,6},{6,4},{8,10},{10,8},{12,14},{14,12},{16,18},{18,... | collective-permute-start | bytes 17694728 | tf_op jit(solution)/shard_map/ppermute | solution.py:319
  486.2 29.7 %collective-permute-start.3 = (bf16[256,1536]{0,1:T(8,128)(2,1)}, bf16[256,1536]{0,1:T(8,128)(2,1)}, u32[]{:S(2)}, u32[]{:S(2)}) collective-permute-start(bf16[256,1536]{0,1:T(8,128)(2,1)} %dynamic-slice_convert_fusion.4), channel_id=1, source_target_pairs={{0,1},{1,0},{2,3},{3,2},{4,5},{5,4},{6,7},{7,6},{8,9},{9,8},{10,11... | collective-permute-start | bytes 2359304 | tf_op jit(solution)/shard_map/ppermute | solution.py:289
  495.2 10.9 %collective-permute-start.7 = (f32[2,1536]{1,0:T(2,128)S(1)}, f32[2,1536]{1,0:T(2,128)S(1)}, u32[]{:S(2)}, u32[]{:S(2)}) collective-permute-start(f32[2,1536]{1,0:T(2,128)S(1)} %pad_maximum_fusion.15), channel_id=1, source_target_pairs={{0,1},{1,0},{2,3},{3,2},{4,5},{5,4},{6,7},{7,6},{8,9},{9,8},{10,11... | collective-permute-start | bytes 36872 | tf_op jit(solution)/shard_map/ppermute | solution.py:333
  496.8 11.9 %copy-start.54 = (bf16[512,4,64]{0,2,1:T(8,128)(2,1)S(1)}, bf16[512,4,64]{0,2,1:T(8,128)(2,1)}, u32[]{:S(2)}) copy-start(bf16[512,4,64]{0,2,1:T(8,128)(2,1)} %fusion.61) | copy-start | bytes 786436
  496.8 11.9 %copy-start.56 = (bf16[512,4,64]{0,2,1:T(8,128)(2,1)S(1)}, bf16[512,4,64]{0,2,1:T(8,128)(2,1)}, u32[]{:S(2)}) copy-start(bf16[512,4,64]{0,2,1:T(8,128)(2,1)} %reduce_sum.148) | copy-start | bytes 786436
  498.3 10.5 %copy-start.31 = (bf16[512,1536]{0,1:T(8,128)(2,1)S(1)}, bf16[512,1536]{0,1:T(8,128)(2,1)}, u32[]{:S(2)}) copy-start(bf16[512,1536]{0,1:T(8,128)(2,1)} %copy-done.30) | copy-start | bytes 4718596
  498.3 10.5 %copy-start.40 = (bf16[512,12,64]{0,2,1:T(8,128)(2,1)S(1)}, bf16[512,12,64]{0,2,1:T(8,128)(2,1)}, u32[]{:S(2)}) copy-start(bf16[512,12,64]{0,2,1:T(8,128)(2,1)} %copy-done.39) | copy-start | bytes 2359300
  498.3 10.4 %copy-start.67 = (f32[512]{0:T(512)S(1)}, f32[512]{0:T(512)}, u32[]{:S(2)}) copy-start(f32[512]{0:T(512)} %copy-done.66) | copy-start | bytes 6148
  506.2 1.2 collective-permute-start.8
  506.4 8.6 collective-permute-start.16
  507.5 3.8 collective-permute-start.9
  508.8 13.1 %slice-start.7 = ((s8[11796480]{0:T(1024)(128)(4,1)}), s8[4194304]{0:T(1024)(128)(4,1)S(1)}, s32[]{:S(2)}) async-start(s8[11796480]{0:T(1024)(128)(4,1)} %bitcast.233), calls=%async_computation.10 | async-start | bytes 8388608
  508.8 13.1 %slice-start.8 = ((s8[11796480]{0:T(1024)(128)(4,1)}), s8[4194304]{0:T(1024)(128)(4,1)S(1)}, s32[]{:S(2)}) async-start(s8[11796480]{0:T(1024)(128)(4,1)} %bitcast.233), calls=%async_computation.11 | async-start | bytes 8388608
  511.2 3.8 collective-permute-start.10
  515.0 82.5 %collective-permute-start.28 = (bf16[8,3,5,96,256]{4,3,2,1,0:T(8,128)(2,1)}, bf16[8,3,5,96,256]{4,3,2,1,0:T(8,128)(2,1)}, u32[]{:S(2)}, u32[]{:S(2)}) collective-permute-start(bf16[8,3,5,96,256]{4,3,2,1,0:T(8,128)(2,1)} %dynamic-slice_bitcast_fusion.1), channel_id=1, source_target_pairs={{0,2},{2,0},{4,6},{6,4},{8,10},{10,8},{12,14},{14,12},{16,18},{18,... | collective-permute-start | bytes 17694728 | tf_op jit(solution)/shard_map/ppermute | solution.py:319
  515.0 21.9 %collective-permute-start.12 = (bf16[8,96,1280]{2,1,0:T(8,128)(2,1)}, bf16[8,96,1280]{2,1,0:T(8,128)(2,1)}, u32[]{:S(2)}, u32[]{:S(2)}) collective-permute-start(bf16[8,96,1280]{2,1,0:T(8,128)(2,1)} %dynamic-slice_bitcast_fusion.8), channel_id=1, source_target_pairs={{0,2},{2,0},{4,6},{6,4},{8,10},{10,8},{12,14},{14,12},{16,18},{18,... | collective-permute-start | bytes 5898248 | tf_op jit(solution)/shard_map/ppermute | solution.py:319
  515.9 4.8 collective-permute-start.11
  520.7 14.0 %collective-permute-start.17 = (bf16[4,96,768]{2,1,0:T(8,128)(2,1)S(1)}, bf16[4,96,768]{2,1,0:T(8,128)(2,1)S(1)}, u32[]{:S(2)}, u32[]{:S(2)}) collective-permute-start(bf16[4,96,768]{2,1,0:T(8,128)(2,1)S(1)} %dynamic-slice_bitcast_fusion.15), channel_id=1, source_target_pairs={{0,4},{2,6},{4,0},{6,2},{8,12},{10,14},{12,8},{14,10},{16,20},{18,... | collective-permute-start | bytes 1769480 | tf_op jit(solution)/shard_map/ppermute | solution.py:319
  535.5 73.8 %collective-permute-start.32 = (bf16[8,3,5,96,256]{4,3,2,1,0:T(8,128)(2,1)}, bf16[8,3,5,96,256]{4,3,2,1,0:T(8,128)(2,1)}, u32[]{:S(2)}, u32[]{:S(2)}) collective-permute-start(bf16[8,3,5,96,256]{4,3,2,1,0:T(8,128)(2,1)} %dynamic-slice_bitcast_fusion), channel_id=1, source_target_pairs={{0,2},{2,0},{4,6},{6,4},{8,10},{10,8},{12,14},{14,12},{16,18},{18,... | collective-permute-start | bytes 17694728 | tf_op jit(solution)/shard_map/ppermute | solution.py:319
  537.8 9.4 collective-permute-start.18
  539.3 9.1 copy-start.13
  539.3 9.1 copy-start.18
  542.0 10.3 %copy-start.7 = (bf16[8,96,1280]{2,1,0:T(8,128)(2,1)}, bf16[8,96,1280]{2,1,0:T(8,128)(2,1)S(1)}, u32[]{:S(2)}) copy-start(bf16[8,96,1280]{2,1,0:T(8,128)(2,1)S(1)} %fusion.15) | copy-start | bytes 5898244
  547.2 23.6 %collective-permute-start.13 = (bf16[4,96,1280]{2,1,0:T(8,128)(2,1)}, bf16[4,96,1280]{2,1,0:T(8,128)(2,1)}, u32[]{:S(2)}, u32[]{:S(2)}) collective-permute-start(bf16[4,96,1280]{2,1,0:T(8,128)(2,1)} %dynamic-slice_bitcast_fusion.14), channel_id=1, source_target_pairs={{0,4},{2,6},{4,0},{6,2},{8,12},{10,14},{12,8},{14,10},{16,20},{18,... | collective-permute-start | bytes 2949128 | tf_op jit(solution)/shard_map/ppermute | solution.py:319
  555.5 17.8 %copy-start.8 = (bf16[8,96,1280]{2,1,0:T(8,128)(2,1)S(1)}, bf16[8,96,1280]{2,1,0:T(8,128)(2,1)}, u32[]{:S(2)}) copy-start(bf16[8,96,1280]{2,1,0:T(8,128)(2,1)} %copy-done.7) | copy-start | bytes 5898244
  570.8 48.2 %collective-permute-start.19 = (bf16[1,96,768]{2,1,0:T(8,128)(2,1)S(1)}, bf16[1,96,768]{2,1,0:T(8,128)(2,1)S(1)}, u32[]{:S(2)}, u32[]{:S(2)}) collective-permute-start(bf16[1,96,768]{2,1,0:T(8,128)(2,1)S(1)} %constant_dynamic-slice_fusion.4), channel_id=1, source_target_pairs={{0,16},{2,18},{4,20},{6,22},{8,24},{10,26},{12,28},{14,30},{16,0},... | collective-permute-start | bytes 442376 | tf_op jit(solution)/shard_map/ppermute | solution.py:319
  574.7 42.5 %collective-permute-start.14 = (bf16[2,96,1280]{2,1,0:T(8,128)(2,1)S(1)}, bf16[2,96,1280]{2,1,0:T(8,128)(2,1)S(1)}, u32[]{:S(2)}, u32[]{:S(2)}) collective-permute-start(bf16[2,96,1280]{2,1,0:T(8,128)(2,1)S(1)} %dynamic-slice_bitcast_fusion.16), channel_id=1, source_target_pairs={{0,8},{2,10},{4,12},{6,14},{8,0},{10,2},{12,4},{14,6},{16,24},{18,... | collective-permute-start | bytes 1474568 | tf_op jit(solution)/shard_map/ppermute | solution.py:319
  586.6 67.1 %collective-permute-start.21 = (bf16[4,3,5,96,256]{4,3,2,1,0:T(8,128)(2,1)}, bf16[4,3,5,96,256]{4,3,2,1,0:T(8,128)(2,1)}, u32[]{:S(2)}, u32[]{:S(2)}) collective-permute-start(bf16[4,3,5,96,256]{4,3,2,1,0:T(8,128)(2,1)} %dynamic-slice_bitcast_fusion.7), channel_id=1, source_target_pairs={{0,4},{2,6},{4,0},{6,2},{8,12},{10,14},{12,8},{14,10},{16,20},{18,... | collective-permute-start | bytes 8847368 | tf_op jit(solution)/shard_map/ppermute | solution.py:319
  597.5 119.4 %collective-permute-start.25 = (bf16[4,3,5,96,256]{4,3,2,1,0:T(8,128)(2,1)}, bf16[4,3,5,96,256]{4,3,2,1,0:T(8,128)(2,1)}, u32[]{:S(2)}, u32[]{:S(2)}) collective-permute-start(bf16[4,3,5,96,256]{4,3,2,1,0:T(8,128)(2,1)} %dynamic-slice_bitcast_fusion.6), channel_id=1, source_target_pairs={{0,4},{2,6},{4,0},{6,2},{8,12},{10,14},{12,8},{14,10},{16,20},{18,... | collective-permute-start | bytes 8847368 | tf_op jit(solution)/shard_map/ppermute | solution.py:319
  609.3 170.8 %collective-permute-start.29 = (bf16[4,3,5,96,256]{4,3,2,1,0:T(8,128)(2,1)}, bf16[4,3,5,96,256]{4,3,2,1,0:T(8,128)(2,1)}, u32[]{:S(2)}, u32[]{:S(2)}) collective-permute-start(bf16[4,3,5,96,256]{4,3,2,1,0:T(8,128)(2,1)} %dynamic-slice_bitcast_fusion.5), channel_id=1, source_target_pairs={{0,4},{2,6},{4,0},{6,2},{8,12},{10,14},{12,8},{14,10},{16,20},{18,... | collective-permute-start | bytes 8847368 | tf_op jit(solution)/shard_map/ppermute | solution.py:319
  617.2 223.2 %collective-permute-start.33 = (bf16[4,3,5,96,256]{4,3,2,1,0:T(8,128)(2,1)S(1)}, bf16[4,3,5,96,256]{4,3,2,1,0:T(8,128)(2,1)S(1)}, u32[]{:S(2)}, u32[]{:S(2)}) collective-permute-start(bf16[4,3,5,96,256]{4,3,2,1,0:T(8,128)(2,1)S(1)} %dynamic-slice_bitcast_fusion.4), channel_id=1, source_target_pairs={{0,4},{2,6},{4,0},{6,2},{8,12},{10,14},{12,8},{14,10},{16,20},{18,... | collective-permute-start | bytes 8847368 | tf_op jit(solution)/shard_map/ppermute | solution.py:319
  619.0 11.1 %collective-permute-start.15 = (bf16[1,96,1280]{2,1,0:T(8,128)(2,1)S(1)}, bf16[1,96,1280]{2,1,0:T(8,128)(2,1)S(1)}, u32[]{:S(2)}, u32[]{:S(2)}) collective-permute-start(bf16[1,96,1280]{2,1,0:T(8,128)(2,1)S(1)} %constant_dynamic-slice_fusion.5), channel_id=1, source_target_pairs={{0,16},{2,18},{4,20},{6,22},{8,24},{10,26},{12,28},{14,30},{16,0},... | collective-permute-start | bytes 737288 | tf_op jit(solution)/shard_map/ppermute | solution.py:319
  630.1 86.8 %slice-start = ((s8[5898240]{0:T(1024)(128)(4,1)}), s8[4194304]{0:T(1024)(128)(4,1)S(1)}, s32[]{:S(2)}) async-start(s8[5898240]{0:T(1024)(128)(4,1)} %bitcast.221), calls=%async_computation.3 | async-start | bytes 8388608
  630.8 86.0 %slice-start.1 = ((s8[5898240]{0:T(1024)(128)(4,1)}), s8[1703936]{0:T(1024)(128)(4,1)S(1)}, s32[]{:S(2)}) async-start(s8[5898240]{0:T(1024)(128)(4,1)} %bitcast.221), calls=%async_computation.4 | async-start | bytes 3407872
  657.5 122.6 %slice-start.2 = ((s8[5898240]{0:T(1024)(128)(4,1)}), s8[4194304]{0:T(1024)(128)(4,1)S(1)}, s32[]{:S(2)}) async-start(s8[5898240]{0:T(1024)(128)(4,1)} %bitcast.225), calls=%async_computation.5 | async-start | bytes 8388608
  657.6 122.5 %slice-start.3 = ((s8[5898240]{0:T(1024)(128)(4,1)}), s8[1703936]{0:T(1024)(128)(4,1)S(1)}, s32[]{:S(2)}) async-start(s8[5898240]{0:T(1024)(128)(4,1)} %bitcast.225), calls=%async_computation.6 | async-start | bytes 3407872
  657.6 185.3 %collective-permute-start.22 = (bf16[2,3,5,96,256]{4,3,2,1,0:T(8,128)(2,1)S(1)}, bf16[2,3,5,96,256]{4,3,2,1,0:T(8,128)(2,1)}, u32[]{:S(2)}, u32[]{:S(2)}) collective-permute-start(bf16[2,3,5,96,256]{4,3,2,1,0:T(8,128)(2,1)S(1)} %dynamic-slice_bitcast_fusion.12), channel_id=1, source_target_pairs={{0,8},{2,10},{4,12},{6,14},{8,0},{10,2},{12,4},{14,6},{16,24},{18,... | collective-permute-start | bytes 4423688 | tf_op jit(solution)/shard_map/ppermute | solution.py:319
  720.0 125.5 %collective-permute-start.26 = (bf16[2,3,5,96,256]{4,3,2,1,0:T(8,128)(2,1)S(1)}, bf16[2,3,5,96,256]{4,3,2,1,0:T(8,128)(2,1)}, u32[]{:S(2)}, u32[]{:S(2)}) collective-permute-start(bf16[2,3,5,96,256]{4,3,2,1,0:T(8,128)(2,1)S(1)} %dynamic-slice_bitcast_fusion.11), channel_id=1, source_target_pairs={{0,8},{2,10},{4,12},{6,14},{8,0},{10,2},{12,4},{14,6},{16,24},{18,... | collective-permute-start | bytes 4423688 | tf_op jit(solution)/shard_map/ppermute | solution.py:319
  783.2 66.7 %collective-permute-start.30 = (bf16[2,3,5,96,256]{4,3,2,1,0:T(8,128)(2,1)S(1)}, bf16[2,3,5,96,256]{4,3,2,1,0:T(8,128)(2,1)}, u32[]{:S(2)}, u32[]{:S(2)}) collective-permute-start(bf16[2,3,5,96,256]{4,3,2,1,0:T(8,128)(2,1)S(1)} %dynamic-slice_bitcast_fusion.10), channel_id=1, source_target_pairs={{0,8},{2,10},{4,12},{6,14},{8,0},{10,2},{12,4},{14,6},{16,24},{18,... | collective-permute-start | bytes 4423688 | tf_op jit(solution)/shard_map/ppermute | solution.py:319
  841.7 59.4 %collective-permute-start.34 = (bf16[2,3,5,96,256]{4,3,2,1,0:T(8,128)(2,1)S(1)}, bf16[2,3,5,96,256]{4,3,2,1,0:T(8,128)(2,1)S(1)}, u32[]{:S(2)}, u32[]{:S(2)}) collective-permute-start(bf16[2,3,5,96,256]{4,3,2,1,0:T(8,128)(2,1)S(1)} %dynamic-slice_bitcast_fusion.9), channel_id=1, source_target_pairs={{0,8},{2,10},{4,12},{6,14},{8,0},{10,2},{12,4},{14,6},{16,24},{18,... | collective-permute-start | bytes 4423688 | tf_op jit(solution)/shard_map/ppermute | solution.py:319
  844.9 56.9 %collective-permute-start.23 = (bf16[1,3,5,96,256]{4,3,2,1,0:T(8,128)(2,1)S(1)}, bf16[1,3,5,96,256]{4,3,2,1,0:T(8,128)(2,1)S(1)}, u32[]{:S(2)}, u32[]{:S(2)}) collective-permute-start(bf16[1,3,5,96,256]{4,3,2,1,0:T(8,128)(2,1)S(1)} %constant_dynamic-slice_fusion.3), channel_id=1, source_target_pairs={{0,16},{2,18},{4,20},{6,22},{8,24},{10,26},{12,28},{14,30},{16,0},... | collective-permute-start | bytes 2211848 | tf_op jit(solution)/shard_map/ppermute | solution.py:319
  847.4 96.8 %collective-permute-start.27 = (bf16[1,3,5,96,256]{4,3,2,1,0:T(8,128)(2,1)S(1)}, bf16[1,3,5,96,256]{4,3,2,1,0:T(8,128)(2,1)S(1)}, u32[]{:S(2)}, u32[]{:S(2)}) collective-permute-start(bf16[1,3,5,96,256]{4,3,2,1,0:T(8,128)(2,1)S(1)} %constant_dynamic-slice_fusion.2), channel_id=1, source_target_pairs={{0,16},{2,18},{4,20},{6,22},{8,24},{10,26},{12,28},{14,30},{16,0},... | collective-permute-start | bytes 2211848 | tf_op jit(solution)/shard_map/ppermute | solution.py:319
  851.9 108.1 %collective-permute-start.31 = (bf16[1,3,5,96,256]{4,3,2,1,0:T(8,128)(2,1)S(1)}, bf16[1,3,5,96,256]{4,3,2,1,0:T(8,128)(2,1)S(1)}, u32[]{:S(2)}, u32[]{:S(2)}) collective-permute-start(bf16[1,3,5,96,256]{4,3,2,1,0:T(8,128)(2,1)S(1)} %constant_dynamic-slice_fusion.1), channel_id=1, source_target_pairs={{0,16},{2,18},{4,20},{6,22},{8,24},{10,26},{12,28},{14,30},{16,0},... | collective-permute-start | bytes 2211848 | tf_op jit(solution)/shard_map/ppermute | solution.py:319
  901.7 70.3 %collective-permute-start.35 = (bf16[1,3,5,96,256]{4,3,2,1,0:T(8,128)(2,1)S(1)}, bf16[1,3,5,96,256]{4,3,2,1,0:T(8,128)(2,1)S(1)}, u32[]{:S(2)}, u32[]{:S(2)}) collective-permute-start(bf16[1,3,5,96,256]{4,3,2,1,0:T(8,128)(2,1)S(1)} %constant_dynamic-slice_fusion), channel_id=1, source_target_pairs={{0,16},{2,18},{4,20},{6,22},{8,24},{10,26},{12,28},{14,30},{16,0},... | collective-permute-start | bytes 2211848 | tf_op jit(solution)/shard_map/ppermute | solution.py:319
  (57 other events, 206.3 us)
Sparse Core Ops, SparseCore 0:
  10.9 64.1 all-gather.5
  76.6 119.8 all-gather.9
  198.1 121.0 all-gather.7
